TPU v7x, 256 devices: a whole 4x4x8 slice. The times are simulated.
256 devices in a mesh: slab: 32 (over z, y), energy: 8 (over x, core).
Axes of the slice: x: 4, y: 4, z: 8, core: 2. Of those that a mesh axis runs over, the one named last changes fastest.
Arguments:
- green: bfloat16 [8, 32, 3, 2, 384, 384], P('energy', 'slab'), may hold values from -0.3125 to 0.3125
- sigma: bfloat16 [8, 32, 3, 2, 384, 384], P('energy', 'slab'), may hold values from -4 to 4
- phonon: bfloat16 [8, 32, 2, 384, 384], P('energy', 'slab'), may hold values from -4 to 4
- pair_off: int32 [32, 3], replicated, may hold values from -2 to 2, as said below
- pair_count: int32 [32], replicated, may hold values from 1 to 3, as said below
- pair_range: int32 [32, 3], replicated, may hold values from 96 to 384, as said below
Outputs:
- lesser: float32 [8, 32, 2, 384, 384], P('energy', 'slab')
Inputs may be any that keep to these rules, and one draw needn't show every extreme that they name: The partner slab k + pair_off[k, q] lies inside the grid. `pair_count`: some slab has 3 live slots. `pair_range`: a multiple of 96; some pair couples all 384 orbitals.
All inputs are finite; a program needn't handle non-finite values.
Results may differ from a plain program's by a relative error of at most 0.0035.
Values may be sent and summed in bfloat16 or wider, within the bound.
A program may use at most 64 MiB of HBM per device.

v0:
```python
import jax
import jax.numpy as jnp
from jax import lax
from jax.sharding import PartitionSpec as P


def from_behind(value, axis, steps):
    count = lax.axis_size(axis)
    leading, last = (max(0, -steps), min(count, count - steps))
    return lax.ppermute(value, axis, [(source, source + steps) for source in range(leading, last)])


def extended_2(block, sides, width):
    for axis, dim in sides:
        count = lax.axis_size(axis)
        forward = [(i, i + 1) for i in range(count - 1)]
        backward = [(target, source) for source, target in forward]
        low = lax.ppermute(
            lax.slice_in_dim(block, block.shape[dim] - width, None, axis=dim), axis, forward
        )
        high = lax.ppermute(lax.slice_in_dim(block, 0, width, axis=dim), axis, backward)
        block = jnp.concatenate([low, block, high], axis=dim)
    return block


def conj_sum(source, chosen):
    layout = (((0, 2), (0, 2)), ((), ()))

    def pair_dot(left, right):
        return lax.dot_general(left, right, layout, preferred_element_type=jnp.float32)

    real = pair_dot(source[:, 0], chosen[:, 0]) + pair_dot(source[:, 1], chosen[:, 1])
    imag = pair_dot(source[:, 1], chosen[:, 0]) - pair_dot(source[:, 0], chosen[:, 1])
    return (real, imag)


def complex_times(left, real, imag):
    first = jnp.dot(left[0], real, preferred_element_type=jnp.float32) - jnp.dot(
        left[1], imag, preferred_element_type=jnp.float32
    )
    second = jnp.dot(left[0], imag, preferred_element_type=jnp.float32) + jnp.dot(
        left[1], real, preferred_element_type=jnp.float32
    )
    return jnp.stack([first, second])


def slab_term(green_row, source, other, row_slab, diag_at, pair_off, pair_count):
    slab_total = pair_off.shape[0]
    slots = pair_off.shape[1]
    clipped = jnp.clip(other, 0, slab_total - 1)
    offsets = lax.dynamic_index_in_dim(pair_off, clipped, 0, keepdims=False)
    count = lax.dynamic_index_in_dim(pair_count, clipped, 0, keepdims=False)
    place = clipped + offsets - row_slab + 1
    slot_ids = jnp.arange(slots, dtype=jnp.int32)
    usable = (place >= 0) & (place <= 2) & (slot_ids < count)
    pick = jnp.concatenate([jnp.clip(place, 0, 2), jnp.full((1,), diag_at, jnp.int32)])
    keep = jnp.concatenate([usable, jnp.ones((1,), bool)]).astype(jnp.bfloat16)
    chosen = jnp.take(green_row, pick, axis=0) * keep[:, None, None, None]
    real, imag = conj_sum(source, chosen)
    return complex_times(green_row[diag_at], real.astype(jnp.bfloat16), imag.astype(jnp.bfloat16))


def body(green, sigma, phonon, pair_off, pair_count, pair_range):
    slab_count = green.shape[1]
    width = green.shape[-1]
    first_slab = lax.axis_index("slab") * slab_count
    sides = [from_behind(phonon, "energy", shift_by) for shift_by in (1, -1)]
    phonon_mix = (0.5 * (sides[0].astype(jnp.float32) + sides[1].astype(jnp.float32))).astype(
        jnp.bfloat16
    )
    local_range = lax.dynamic_slice_in_dim(pair_range, first_slab, slab_count, 0)
    positions = jnp.arange(width, dtype=jnp.int32)
    inside = positions[None, None, :] < local_range[:, :, None]
    square = inside[:, :, :, None] & inside[:, :, None, :]
    masked = jnp.where(square[:, :, None], sigma[0], jnp.zeros((), jnp.bfloat16))
    stacked = jnp.concatenate([masked, phonon_mix[0][:, None]], axis=1)
    extended = extended_2(stacked, (("slab", 0),), 1)
    row_slab = first_slab + 0
    green_row = green[0, 0]
    running = jnp.zeros((2, width, width), jnp.float32)
    for delta in (-1, 0, 1):
        running = running + slab_term(
            green_row,
            extended[1 + delta],
            row_slab + delta,
            row_slab,
            delta + 1,
            pair_off,
            pair_count,
        )
    results = [running]
    return jnp.stack(results)[None]


def solution(mesh):
    in_specs = (
        P("energy", "slab", None, None, None, None),
        P("energy", "slab", None, None, None, None),
        P("energy", "slab", None, None, None),
        P(),
        P(),
        P(),
    )
    out_specs = P("energy", "slab", None, None, None)
    return jax.shard_map(body, mesh=mesh, in_specs=in_specs, out_specs=out_specs, check_vma=False)
```

profile of v0, /device:TPU:130, one launch (start us, length us, event | category | flops | bytes accessed | tf_op | source)
XLA Modules:
  0.0 112.8 jit_solution(13357998503600026632)
XLA Ops:
  0.0 2.0 %collective-permute-start = (bf16[1,1,2,384,384]{4,3,1,2,0:T(8,128)(2,1)}, bf16[1,1,2,384,384]{4,3,1,2,0:T(8,128)(2,1)}, u32[]{:S(2)}, u32[]{:S(2)}) collective-permute-start(bf16[1,1,2,384,384]{4,3,1,2,0:T(8,128)(2,1)} %bitcast.181), channel_id=1, source_target_pairs={{0,1},{1,2},{2,3},{3,4},{4,5},{5,6},{6,7},{8,9},{9,10},{10,11},{11... | collective-permute-start | bytes 1769480 | tf_op jit(solution)/shard_map/ppermute | solution.py:10
  2.1 3.6 %collective-permute-start.1 = (bf16[1,1,2,384,384]{4,3,1,2,0:T(8,128)(2,1)}, bf16[1,1,2,384,384]{4,3,1,2,0:T(8,128)(2,1)}, u32[]{:S(2)}, u32[]{:S(2)}) collective-permute-start(bf16[1,1,2,384,384]{4,3,1,2,0:T(8,128)(2,1)} %bitcast.182), channel_id=1, source_target_pairs={{1,0},{2,1},{3,2},{4,3},{5,4},{6,5},{7,6},{9,8},{10,9},{11,10},{12... | collective-permute-start | bytes 1769480 | tf_op jit(solution)/shard_map/ppermute | solution.py:10
  5.7 1.5 %and_reduce_fusion = (pred[3]{0:T(512)(128)(4,1)S(1)}, pred[3]{0:T(512)(128)(4,1)S(1)}, pred[3]{0:T(512)(128)(4,1)}) fusion(s32[]{:T(128)S(6)} %axis_index.15, s32[32,3]{0,1:T(4,128)} %param.11, s32[]{:T(128)S(6)} %min.39, s32[]{:T(128)S(6)} %min.36, s32[]{:T(128)S(6)} %min.32), kind=kLoop, calls=%fused_computation.116 | loop fusion | flops 54 | bytes 3629 | tf_op jit(solution)/shard_map/and | solution.py:55
  7.2 1.0 clamp_reduce_fusion
  8.2 1.4 %fusion.56 = (s32[1]{0:T(128)}, s32[1]{0:T(128)}, s32[1]{0:T(128)}) fusion(s32[32]{0:T(128)} %param.12, s32[]{:T(128)S(6)} %min.39, s32[]{:T(128)S(6)} %min.32, s32[]{:T(128)S(6)} %min.36), kind=kLoop, calls=%fused_computation.123 | loop fusion | bytes 36 | tf_op jit(solution)/shard_map/jit(dynamic_index_in_dim)/dynamic_slice | solution.py:52
  9.7 0.7 compare_and_fusion
  10.6 1.0 broadcast_and_fusion
  11.8 1.7 %compare_and_fusion.3 = (pred[3]{0:T(512)(128)(4,1)S(1)}, pred[3]{0:T(512)(128)(4,1)}) fusion(pred[3]{0:T(512)(128)(4,1)S(1)} %get-tuple-element.6, s32[]{:T(128)} %bitcast.38, pred[3]{0:T(512)(128)(4,1)S(1)} %get-tuple-element.7, s32[]{:T(128)} %bitcast.22), kind=kLoop, calls=%fused_computation.119 | loop fusion | flops 12 | bytes 20 | tf_op jit(solution)/shard_map/and | solution.py:55
  13.5 0.6 fusion.54
  14.0 3.9 %gather_fusion.2 = bf16[4,2,384,384]{3,2,1,0:T(8,128)(2,1)} fusion(bf16[3,2,384,384]{3,2,1,0:T(8,128)(2,1)} %bitcast.174, s32[1024]{0:T(1024)S(1)} %pad_clamp_fusion), kind=kCustom, calls=%fused_computation.2.clone | custom fusion | bytes 4718608 | tf_op jit(solution)/shard_map/jit(_take)/gather | solution.py:58
  17.9 1.5 %bitcast_select_fusion = bf16[1,3,2,384,384]{4,3,1,2,0:T(8,128)(2,1)S(1)} fusion(bf16[1,1,3,2,384,384]{5,4,3,2,1,0:T(8,128)(2,1)S(1)} %copy-done.6, pred[3,384,384]{2,1,0:T(8,128)(4,1)} %broadcast_and_fusion), kind=kLoop, calls=%fused_computation.10 | loop fusion | flops 884736 | bytes 3981312 | tf_op jit(solution)/shard_map/jit(_where)/select_n | solution.py:75
  19.7 1.8 %fusion = bf16[4,2,384,384]{3,2,0,1:T(8,128)(2,1)} fusion(bf16[4,2,384,384]{3,2,1,0:T(8,128)(2,1)S(1)} %copy-done.2, pred[4]{0:T(512)(128)(4,1)S(1)} %copy-done.7, bf16[4]{0:T(256)(128)(2,1)S(1)} %copy-done.8), kind=kLoop, calls=%fused_computation.5 | loop fusion | flops 2359296 | bytes 4718604 | tf_op jit(solution)/shard_map/mul | solution.py:58
  21.6 0.6 fusion.53
  22.1 2.3 %gather_fusion.1 = bf16[4,2,384,384]{3,2,1,0:T(8,128)(2,1)} fusion(bf16[3,2,384,384]{3,2,1,0:T(8,128)(2,1)S(1)} %bitcast.175, s32[1024]{0:T(1024)S(1)} %pad_clamp_fusion.1), kind=kCustom, calls=%fused_computation.1.clone | custom fusion | bytes 4718608 | tf_op jit(solution)/shard_map/jit(_take)/gather | solution.py:58
  24.5 1.3 %compare_and_fusion.5 = pred[3]{0:T(512)(128)(4,1)S(1)} fusion(pred[3]{0:T(512)(128)(4,1)} %get-tuple-element.8, s32[]{:T(128)} %bitcast.6), kind=kLoop, calls=%fused_computation.121 | loop fusion | flops 6 | bytes 10 | tf_op jit(solution)/shard_map/and | solution.py:55
  25.8 3.5 %fusion.1 = bf16[4,2,384,384]{3,2,0,1:T(8,128)(2,1)} fusion(bf16[4,2,384,384]{3,2,1,0:T(8,128)(2,1)} %gather_fusion.1, pred[4]{0:T(512)(128)(4,1)} %get-tuple-element.23, bf16[4]{0:T(256)(128)(2,1)} %fusion.53), kind=kLoop, calls=%fused_computation.7 | loop fusion | flops 2359296 | bytes 4718604 | tf_op jit(solution)/shard_map/mul | solution.py:58
  29.2 1.4 %multiply_convert_fusion = bf16[1,1,2,384,384]{4,3,1,2,0:T(8,128)(2,1)S(1)} fusion(bf16[1,1,2,384,384]{4,3,1,2,0:T(8,128)(2,1)} %collective-permute-done.1, bf16[1,1,2,384,384]{4,3,1,2,0:T(8,128)(2,1)} %collective-permute-done), kind=kLoop, calls=%fused_computation.61 | loop fusion | flops 1474560 | bytes 1769472 | tf_op jit(solution)/shard_map/convert_element_type | solution.py:68
  30.7 2.6 %fusion.55 = (bf16[4,2,384,384]{3,2,0,1:T(8,128)(2,1)}, bf16[1,4,2,384,384]{4,3,1,2,0:T(8,128)(2,1)}) fusion(bf16[1,1,2,384,384]{4,3,1,2,0:T(8,128)(2,1)S(1)} %multiply_convert_fusion, bf16[1,3,2,384,384]{4,3,1,2,0:T(8,128)(2,1)S(1)} %bitcast_select_fusion), kind=kLoop, calls=%fused_computation.122 | loop fusion | flops 1179648 | bytes 7077888 | tf_op jit(solution)/shard_map/squeeze | solution.py:84
  33.3 4.5 %collective-permute-start.3 = (bf16[1,4,2,384,384]{4,3,1,2,0:T(8,128)(2,1)}, bf16[1,4,2,384,384]{4,3,1,2,0:T(8,128)(2,1)}, u32[]{:S(2)}, u32[]{:S(2)}) collective-permute-start(bf16[1,4,2,384,384]{4,3,1,2,0:T(8,128)(2,1)} %get-tuple-element.19), channel_id=1, source_target_pairs={{8,0},{16,8},{24,16},{32,24},{40,32},{48,40},{56,48},{64,56},{72,6... | collective-permute-start | bytes 7077896 | tf_op jit(solution)/shard_map/ppermute | solution.py:21
  37.8 2.4 %gather_fusion = bf16[4,2,384,384]{3,2,1,0:T(8,128)(2,1)} fusion(bf16[3,2,384,384]{3,2,1,0:T(8,128)(2,1)S(1)} %bitcast.176, s32[1024]{0:T(1024)S(1)} %pad_clamp_fusion.2), kind=kCustom, calls=%fused_computation.clone | custom fusion | bytes 4718608 | tf_op jit(solution)/shard_map/jit(_take)/gather | solution.py:58
  40.2 2.2 %fusion.2 = bf16[4,2,384,384]{3,2,0,1:T(8,128)(2,1)S(1)} fusion(bf16[4,2,384,384]{3,2,1,0:T(8,128)(2,1)} %gather_fusion, pred[4]{0:T(512)(128)(4,1)S(1)} %get-tuple-element.16, bf16[4]{0:T(256)(128)(2,1)S(1)} %fusion.52), kind=kLoop, calls=%fused_computation.9 | loop fusion | flops 2359296 | bytes 4718604 | tf_op jit(solution)/shard_map/mul | solution.py:58
  42.4 2.1 %collective-permute-start.2 = (bf16[1,4,2,384,384]{4,3,1,2,0:T(8,128)(2,1)}, bf16[1,4,2,384,384]{4,3,1,2,0:T(8,128)(2,1)S(1)}, u32[]{:S(2)}, u32[]{:S(2)}) collective-permute-start(bf16[1,4,2,384,384]{4,3,1,2,0:T(8,128)(2,1)} %get-tuple-element.19), channel_id=1, source_target_pairs={{0,8},{8,16},{16,24},{24,32},{32,40},{40,48},{48,56},{56,64},{64,7... | collective-permute-start | bytes 7077896 | tf_op jit(solution)/shard_map/ppermute | solution.py:18
  44.6 0.8 convolution_bitcast_fusion.6
  45.4 0.8 fusion.18
  46.2 0.4 fusion.32
  46.6 0.8 convolution_bitcast_fusion.4
  47.4 0.8 fusion.17
  48.2 0.4 fusion.6
  49.0 0.4 fusion.5
  49.4 39.2 %collective-permute-done.3 = bf16[1,4,2,384,384]{4,3,1,2,0:T(8,128)(2,1)} collective-permute-done((bf16[1,4,2,384,384]{4,3,1,2,0:T(8,128)(2,1)}, bf16[1,4,2,384,384]{4,3,1,2,0:T(8,128)(2,1)}, u32[]{:S(2)}, u32[]{:S(2)}) %collective-permute-start.3) | collective-permute-done | bytes 2359328 | tf_op jit(solution)/shard_map/ppermute | solution.py:21
  88.6 2.1 %convolution_bitcast_fusion.2 = f32[384,384]{1,0:T(8,128)S(1)} fusion(bf16[4,2,384,384]{3,2,0,1:T(8,128)(2,1)} %bitcast.36, bf16[4,2,384,384]{3,2,0,1:T(8,128)(2,1)S(1)} %copy-done.4), kind=kOutput, calls=%fused_computation.17 | convolution fusion | flops 452984832 | bytes 2949120 | tf_op jit(solution)/shard_map/dot_general | solution.py:30
  90.6 2.1 %convolution_bitcast_fusion = f32[384,384]{1,0:T(8,128)S(1)} fusion(bf16[4,2,384,384]{3,2,0,1:T(8,128)(2,1)} %bitcast.36, bf16[4,2,384,384]{3,2,0,1:T(8,128)(2,1)S(1)} %copy-done.4), kind=kOutput, calls=%fused_computation.15 | convolution fusion | flops 452984832 | bytes 2949120 | tf_op jit(solution)/shard_map/dot_general | solution.py:30
  92.7 7.9 %collective-permute-done.2 = bf16[1,4,2,384,384]{4,3,1,2,0:T(8,128)(2,1)S(1)} collective-permute-done((bf16[1,4,2,384,384]{4,3,1,2,0:T(8,128)(2,1)}, bf16[1,4,2,384,384]{4,3,1,2,0:T(8,128)(2,1)S(1)}, u32[]{:S(2)}, u32[]{:S(2)}) %collective-permute-start.2) | collective-permute-done | bytes 2359328 | tf_op jit(solution)/shard_map/ppermute | solution.py:18
  100.6 0.8 convolution_bitcast_fusion.10
  101.4 0.8 convolution_bitcast_fusion.8
  102.2 2.1 %fusion.16 = bf16[384,384]{1,0:T(8,128)(2,1)S(1)} fusion(f32[384,384]{1,0:T(8,128)S(1)} %convolution_bitcast_fusion.2, bf16[4,2,384,384]{3,2,0,1:T(8,128)(2,1)} %bitcast.36, bf16[4,2,384,384]{3,2,0,1:T(8,128)(2,1)S(1)} %copy-done.4), kind=kOutput, calls=%fused_computation.42 | convolution fusion | flops 453279744 | bytes 3244032 | tf_op jit(solution)/shard_map/dot_general | solution.py:30
  104.3 0.4 fusion.26
  104.7 2.1 %fusion.15 = bf16[384,384]{1,0:T(8,128)(2,1)S(1)} fusion(f32[384,384]{1,0:T(8,128)S(1)} %convolution_bitcast_fusion, bf16[4,2,384,384]{3,2,0,1:T(8,128)(2,1)S(1)} %copy-done.4, bf16[4,2,384,384]{3,2,0,1:T(8,128)(2,1)} %bitcast.36), kind=kOutput, calls=%fused_computation.41 | convolution fusion | flops 453279744 | bytes 3244032 | tf_op jit(solution)/shard_map/dot_general | solution.py:30
  106.7 0.4 fusion.24
  107.1 0.4 fusion.4
  107.6 0.4 fusion.3
  108.0 0.8 fusion.20
  108.8 0.4 fusion.38
  109.2 0.8 fusion.19
  110.0 0.4 fusion.36
  110.4 0.4 fusion.8
  110.8 0.4 fusion.7
  111.4 1.4 %copy.17 = f32[1,1,2,384,384]{4,3,2,1,0:T(8,128)} copy(f32[1,1,2,384,384]{3,4,2,1,0:T(8,128)S(1)} %fusion.21) | data formatting | bytes 2359296 | tf_op jit(solution)/shard_map/add | solution.py:82
  (31 shorter events, 1.3 us)
Async XLA Ops:
  0.0 10.4 %copy-start = (s32[32,3]{0,1:T(4,128)S(1)}, s32[32,3]{0,1:T(4,128)}, u32[]{:S(2)}) copy-start(s32[32,3]{0,1:T(4,128)} %param.13) | copy-start | bytes 1156
  0.0 29.2 %collective-permute-start = (bf16[1,1,2,384,384]{4,3,1,2,0:T(8,128)(2,1)}, bf16[1,1,2,384,384]{4,3,1,2,0:T(8,128)(2,1)}, u32[]{:S(2)}, u32[]{:S(2)}) collective-permute-start(bf16[1,1,2,384,384]{4,3,1,2,0:T(8,128)(2,1)} %bitcast.181), channel_id=1, source_target_pairs={{0,1},{1,2},{2,3},{3,4},{4,5},{5,6},{6,7},{8,9},{9,10},{10,11},{11... | collective-permute-start | bytes 1769480 | tf_op jit(solution)/shard_map/ppermute | solution.py:10
  2.1 27.2 %collective-permute-start.1 = (bf16[1,1,2,384,384]{4,3,1,2,0:T(8,128)(2,1)}, bf16[1,1,2,384,384]{4,3,1,2,0:T(8,128)(2,1)}, u32[]{:S(2)}, u32[]{:S(2)}) collective-permute-start(bf16[1,1,2,384,384]{4,3,1,2,0:T(8,128)(2,1)} %bitcast.182), channel_id=1, source_target_pairs={{1,0},{2,1},{3,2},{4,3},{5,4},{6,5},{7,6},{9,8},{10,9},{11,10},{12... | collective-permute-start | bytes 1769480 | tf_op jit(solution)/shard_map/ppermute | solution.py:10
  14.0 3.9 %copy-start.6 = (bf16[1,1,3,2,384,384]{5,4,3,2,1,0:T(8,128)(2,1)S(1)}, bf16[1,1,3,2,384,384]{5,4,3,2,1,0:T(8,128)(2,1)}, u32[]{:S(2)}) copy-start(bf16[1,1,3,2,384,384]{5,4,3,2,1,0:T(8,128)(2,1)} %param.9) | copy-start | bytes 5308420
  17.9 1.8 %copy-start.2 = (bf16[4,2,384,384]{3,2,1,0:T(8,128)(2,1)S(1)}, bf16[4,2,384,384]{3,2,1,0:T(8,128)(2,1)}, u32[]{:S(2)}) copy-start(bf16[4,2,384,384]{3,2,1,0:T(8,128)(2,1)} %gather_fusion.2) | copy-start | bytes 7077892
  17.9 1.8 %copy-start.7 = (pred[4]{0:T(512)(128)(4,1)S(1)}, pred[4]{0:T(512)(128)(4,1)}, u32[]{:S(2)}) copy-start(pred[4]{0:T(512)(128)(4,1)} %get-tuple-element.12) | copy-start | bytes 16
  17.9 1.8 %copy-start.8 = (bf16[4]{0:T(256)(128)(2,1)S(1)}, bf16[4]{0:T(256)(128)(2,1)}, u32[]{:S(2)}) copy-start(bf16[4]{0:T(256)(128)(2,1)} %fusion.54) | copy-start | bytes 28
  19.7 1.8 %copy-start.9 = (pred[3]{0:T(512)(128)(4,1)S(1)}, pred[3]{0:T(512)(128)(4,1)}, u32[]{:S(2)}) copy-start(pred[3]{0:T(512)(128)(4,1)} %get-tuple-element.26) | copy-start | bytes 13
  19.7 2.4 %copy-start.1 = (bf16[1,1,3,2,384,384]{5,4,3,2,1,0:T(8,128)(2,1)S(1)}, bf16[1,1,3,2,384,384]{5,4,3,2,1,0:T(8,128)(2,1)}, u32[]{:S(2)}) copy-start(bf16[1,1,3,2,384,384]{5,4,3,2,1,0:T(8,128)(2,1)} %param.8) | copy-start | bytes 5308420
  33.3 55.3 %collective-permute-start.3 = (bf16[1,4,2,384,384]{4,3,1,2,0:T(8,128)(2,1)}, bf16[1,4,2,384,384]{4,3,1,2,0:T(8,128)(2,1)}, u32[]{:S(2)}, u32[]{:S(2)}) collective-permute-start(bf16[1,4,2,384,384]{4,3,1,2,0:T(8,128)(2,1)} %get-tuple-element.19), channel_id=1, source_target_pairs={{8,0},{16,8},{24,16},{32,24},{40,32},{48,40},{56,48},{64,56},{72,6... | collective-permute-start | bytes 7077896 | tf_op jit(solution)/shard_map/ppermute | solution.py:21
  40.2 4.3 %copy-start.3 = (bf16[4,2,384,384]{3,2,0,1:T(8,128)(2,1)S(1)}, bf16[4,2,384,384]{3,2,0,1:T(8,128)(2,1)}, u32[]{:S(2)}) copy-start(bf16[4,2,384,384]{3,2,0,1:T(8,128)(2,1)} %get-tuple-element.18) | copy-start | bytes 7077892
  40.2 4.3 %copy-start.5 = (bf16[4,2,384,384]{3,2,0,1:T(8,128)(2,1)S(1)}, bf16[4,2,384,384]{3,2,0,1:T(8,128)(2,1)}, u32[]{:S(2)}) copy-start(bf16[4,2,384,384]{3,2,0,1:T(8,128)(2,1)} %fusion.1) | copy-start | bytes 7077892
  42.4 58.2 %collective-permute-start.2 = (bf16[1,4,2,384,384]{4,3,1,2,0:T(8,128)(2,1)}, bf16[1,4,2,384,384]{4,3,1,2,0:T(8,128)(2,1)S(1)}, u32[]{:S(2)}, u32[]{:S(2)}) collective-permute-start(bf16[1,4,2,384,384]{4,3,1,2,0:T(8,128)(2,1)} %get-tuple-element.19), channel_id=1, source_target_pairs={{0,8},{8,16},{16,24},{24,32},{32,40},{40,48},{48,56},{56,64},{64,7... | collective-permute-start | bytes 7077896 | tf_op jit(solution)/shard_map/ppermute | solution.py:18
  48.6 40.0 %copy-start.4 = (bf16[4,2,384,384]{3,2,0,1:T(8,128)(2,1)S(1)}, bf16[4,2,384,384]{3,2,0,1:T(8,128)(2,1)}, u32[]{:S(2)}) copy-start(bf16[4,2,384,384]{3,2,0,1:T(8,128)(2,1)} %fusion) | copy-start | bytes 7077892
where the time goes:
time: 113 us
  waiting for transfers between devices  47.1 us (42%)
  other arithmetic  21.8 us (19%)
  matrix products  19.4 us (17%)
  starting transfers between devices  12.2 us (11%)
  local copies, waits for them, and re-layouts  11.9 us (11%)
    ppermute x1, waiting for transfers between devices, extended_2(): lax.ppermute(lax.slice_in_dim(block, 0, width, axis=dim), axis, backward)  39.2 us
    dot_general x12, matrix products, pair_dot(): lax.dot_general(left, right, layout, preferred_element_type=jnp.float32)  14.6 us
    gather x3, local copies, waits for them, and re-layouts, slab_term(): chosen = jnp.take(green_row, pick, axis=0) * keep[:, None, None, None]  8.61 us
    ppermute x1, waiting for transfers between devices, extended_2(): lax.ppermute(lax.slice_in_dim(block, block.shape[dim] - width, None, axis...  7.89 us
    mul x3, other arithmetic, slab_term(): chosen = jnp.take(green_row, pick, axis=0) * keep[:, None, None, None]  7.47 us
    ppermute x2, starting transfers between devices, from_behind(): lax.ppermute(value, axis, [(source, source + steps) for source in range(l...  5.68 us
    and x3, other arithmetic, slab_term(): usable = (place >= 0) & (place <= 2) & (slot_ids < count)  4.52 us
    ppermute x1, starting transfers between devices, extended_2(): lax.ppermute(lax.slice_in_dim(block, 0, width, axis=dim), axis, backward)  4.46 us
  transfers between devices with their start and end apart: 4, of which 2 were waited for; matrix products, arithmetic and copies ran while one was open for 33% of the time, Pallas kernels for 0%

commit v1 on v0

v1 whole, which is shorter than its diff:
```python
import functools

import jax
import jax.numpy as jnp
from jax import lax
from jax.experimental import pallas as pl
from jax.experimental.pallas import tpu as pltpu
from jax.sharding import PartitionSpec as P

MESH = pl.DeviceIdType.MESH
F32 = jnp.float32
BF16 = jnp.bfloat16
TILE = 16
CHUNK = 128


def kernel(
    slabs,
    energies,
    off_ref,
    count_ref,
    range_ref,
    green_hbm,
    sigma_hbm,
    phonon_hbm,
    out_hbm,
    green_v,
    sigma_v,
    phonon_v,
    near_v,
    mine_v,
    left_v,
    right_v,
    b_v,
    a_v,
    y_v,
    part_v,
    acc_v,
    out_v,
    local_sem,
    near_send,
    near_recv,
    send_sem,
    recv_sem,
    out_sem,
):
    k = lax.axis_index("slab")
    e = lax.axis_index("energy")
    width = green_v.shape[-1]
    slots = sigma_v.shape[0]
    chunks = width // CHUNK
    has_left, has_right = k > 0, k < slabs - 1
    has_low, has_high = e > 0, e < energies - 1

    load_phonon = pltpu.make_async_copy(phonon_hbm.at[0, 0], phonon_v, local_sem.at[0])
    load_sigma = pltpu.make_async_copy(sigma_hbm.at[0, 0], sigma_v, local_sem.at[1])
    load_green = pltpu.make_async_copy(green_hbm.at[0, 0], green_v, local_sem.at[2])
    load_phonon.start()
    load_sigma.start()
    load_green.start()

    barrier = pltpu.get_barrier_semaphore()
    sides = (
        (has_left, {"slab": k - 1}),
        (has_right, {"slab": k + 1}),
        (has_low, {"energy": e - 1}),
        (has_high, {"energy": e + 1}),
    )
    for there, who in sides:

        @pl.when(there)
        def _():
            pl.semaphore_signal(barrier, inc=1, device_id=who, device_id_type=MESH)

    peers = 4 - sum((k == end).astype(jnp.int32) for end in (0, slabs - 1))
    peers = peers - sum((e == end).astype(jnp.int32) for end in (0, energies - 1))
    pl.semaphore_wait(barrier, peers)

    def near_copy(slot, target):
        return pltpu.make_async_remote_copy(
            src_ref=phonon_v,
            dst_ref=near_v.at[slot],
            send_sem=near_send.at[slot],
            recv_sem=near_recv.at[slot],
            device_id={"energy": target},
            device_id_type=MESH,
        )

    up, down = near_copy(0, e + 1), near_copy(1, e - 1)
    load_phonon.wait()

    @pl.when(has_high)
    def _():
        up.start()

    @pl.when(has_low)
    def _():
        down.start()

    def pieces(way):
        into = (left_v, right_v)[way]
        target = (k + 1, k - 1)[way]
        plan = [(2 * way, 0, 0, width), (2 * way + 1, 1, 0, width)]
        plan += [(4, 2, c * CHUNK, CHUNK) for c in range(chunks)]
        made = []
        for n, (source, slot, row, rows) in enumerate(plan):
            made.append(
                pltpu.make_async_remote_copy(
                    src_ref=mine_v.at[source, pl.ds(row, rows)],
                    dst_ref=into.at[slot, pl.ds(row, rows)],
                    send_sem=send_sem.at[way, n],
                    recv_sem=recv_sem.at[way, n],
                    device_id={"slab": target},
                    device_id_type=MESH,
                )
            )
        return made

    to_right, to_left = pieces(0), pieces(1)

    def combine(place, offset, with_phonon):
        reach = []
        for q in range(slots):
            live = (q < count_ref[k]) & (off_ref[k, q] == offset)
            reach.append(jnp.where(live, range_ref[k, q], 0))

        def step(t, carry):
            rows = pl.ds(pl.multiple_of(t * TILE, TILE), TILE)
            row_ids = t * TILE + lax.broadcasted_iota(jnp.int32, (TILE, width), 0)
            col_ids = lax.broadcasted_iota(jnp.int32, (TILE, width), 1)
            far = jnp.maximum(row_ids, col_ids)
            for part in range(2):
                if with_phonon:
                    low = near_v[0, part, rows, :].astype(F32)
                    high = near_v[1, part, rows, :].astype(F32)
                    total = (0.5 * (low + high)).astype(BF16).astype(F32)
                else:
                    total = jnp.zeros((TILE, width), F32)
                for q in range(slots):
                    term = sigma_v[q, part, rows, :].astype(F32)
                    total = total + jnp.where(far < reach[q], term, 0.0)
                mine_v[place, rows, part * width : (part + 1) * width] = total.astype(BF16)
            return carry

        lax.fori_loop(0, width // TILE, step, 0)

    def start(there, copies):
        @pl.when(there)
        def _():
            for copy in copies:
                copy.start()

    load_sigma.wait()
    combine(0, 1, False)
    start(has_right, to_right[:1])
    combine(2, -1, False)
    start(has_left, to_left[:1])
    combine(1, 2, False)
    start(has_right, to_right[1:2])
    combine(3, -2, False)
    start(has_left, to_left[1:2])

    for there, buffer in ((has_left, left_v), (has_right, right_v)):

        @pl.when(jnp.logical_not(there))
        def _():
            buffer[...] = jnp.zeros_like(buffer)

    for there, slot in ((has_low, 0), (has_high, 1)):

        @pl.when(jnp.logical_not(there))
        def _():
            near_v[slot] = jnp.zeros_like(near_v[slot])

    load_green.wait()
    for place in range(3):
        for part in range(2):
            turned = green_v[place, part].astype(F32).T
            for again in range(2):
                row = (part + again) % 2
                sign = -1.0 if (part == 1 and row == 0) else 1.0
                b_v[place, row * width : (row + 1) * width, again * width : (again + 1) * width] = (
                    sign * turned
                ).astype(BF16)
    for c in range(chunks):
        for n, place in enumerate((1, 0, 2)):
            for part in range(2):
                at = n * 2 * CHUNK + part * CHUNK
                a_v[c, :, at : at + CHUNK] = green_v[place, part, :, c * CHUNK : (c + 1) * CHUNK]

    @pl.when(has_low)
    def _():
        up.wait_recv()

    @pl.when(has_high)
    def _():
        down.wait_recv()

    combine(4, 0, True)
    start(has_right, to_right[2:])
    start(has_left, to_left[2:])

    def dot(a, b):
        return jnp.dot(a, b, preferred_element_type=F32)

    def put(at, x):
        real = x[:, :width].astype(BF16)
        imag = x[:, width:].astype(BF16)
        y_v[at : at + CHUNK, :width] = real
        y_v[at : at + CHUNK, width:] = imag
        y_v[at + CHUNK : at + 2 * CHUNK, :width] = -imag
        y_v[at + CHUNK : at + 2 * CHUNK, width:] = real

    for c in range(chunks):
        rows = slice(c * CHUNK, (c + 1) * CHUNK)
        x = dot(mine_v[2, rows], b_v[0]) + dot(mine_v[4, rows], b_v[1]) + dot(mine_v[0, rows], b_v[2])
        put(0, x)
        term = dot(a_v[c, :, : 2 * CHUNK], y_v[: 2 * CHUNK])
        acc_v[...] = term if c == 0 else acc_v[...] + term

    def arrived(there, copy):
        @pl.when(there)
        def _():
            copy.wait_recv()

    def blocks(way, slot, place):
        buffer = (left_v, right_v)[way]

        def step(c, carry):
            rows = pl.ds(pl.multiple_of(c * CHUNK, CHUNK), CHUNK)
            term = dot(buffer[slot, rows], b_v[place])
            part_v[way, rows] = term if slot == 0 else part_v[way, rows] + term
            return carry

        lax.fori_loop(0, chunks, step, 0)

    arrived(has_left, to_right[0])
    blocks(0, 0, 1)
    arrived(has_right, to_left[0])
    blocks(1, 0, 1)
    arrived(has_left, to_right[1])
    blocks(0, 1, 2)
    arrived(has_right, to_left[1])
    blocks(1, 1, 0)
    writes = []
    for c in range(chunks):
        rows = slice(c * CHUNK, (c + 1) * CHUNK)
        arrived(has_left, to_right[2 + c])
        put(0, part_v[0, rows] + dot(left_v[2, rows], b_v[0]))
        arrived(has_right, to_left[2 + c])
        put(2 * CHUNK, part_v[1, rows] + dot(right_v[2, rows], b_v[2]))
        if c < chunks - 1:
            acc_v[...] = acc_v[...] + dot(a_v[c, :, 2 * CHUNK :], y_v[...])
        else:
            for m in range(chunks):
                these = slice(m * CHUNK, (m + 1) * CHUNK)
                total = acc_v[these] + dot(a_v[c, these, 2 * CHUNK :], y_v[...])
                for part in range(2):
                    out_v[part, these] = total[:, part * width : (part + 1) * width]
                    write = pltpu.make_async_copy(
                        out_v.at[part, these], out_hbm.at[0, 0, part, these], out_sem.at[m, part]
                    )
                    write.start()
                    writes.append(write)

    @pl.when(has_high)
    def _():
        up.wait_send()

    @pl.when(has_low)
    def _():
        down.wait_send()

    for there, copies in ((has_right, to_right), (has_left, to_left)):

        @pl.when(there)
        def _():
            for copy in copies:
                copy.wait_send()

    for write in writes:
        write.wait()


def solution(mesh):
    slabs, energies = mesh.shape["slab"], mesh.shape["energy"]

    def body(green, sigma, phonon, pair_off, pair_count, pair_range):
        width = green.shape[-1]
        slots = sigma.shape[2]
        chunks = width // CHUNK
        smem = pl.BlockSpec(memory_space=pltpu.SMEM)
        hbm = pl.BlockSpec(memory_space=pl.ANY)
        block = (width, 2 * width)
        return pl.pallas_call(
            functools.partial(kernel, slabs, energies),
            out_shape=jax.ShapeDtypeStruct((1, 1, 2, width, width), F32),
            in_specs=[smem, smem, smem, hbm, hbm, hbm],
            out_specs=hbm,
            scratch_shapes=[
                pltpu.VMEM((3, 2, width, width), BF16),
                pltpu.VMEM((slots, 2, width, width), BF16),
                pltpu.VMEM((2, width, width), BF16),
                pltpu.VMEM((2, 2, width, width), BF16),
                pltpu.VMEM((5,) + block, BF16),
                pltpu.VMEM((3,) + block, BF16),
                pltpu.VMEM((3,) + block, BF16),
                pltpu.VMEM((3, 2 * width, 2 * width), BF16),
                pltpu.VMEM((chunks, width, 6 * CHUNK), BF16),
                pltpu.VMEM((4 * CHUNK, 2 * width), BF16),
                pltpu.VMEM((2,) + block, F32),
                pltpu.VMEM(block, F32),
                pltpu.VMEM((2, width, width), F32),
                pltpu.SemaphoreType.DMA((3,)),
                pltpu.SemaphoreType.DMA((2,)),
                pltpu.SemaphoreType.DMA((2,)),
                pltpu.SemaphoreType.DMA((2, 2 + chunks)),
                pltpu.SemaphoreType.DMA((2, 2 + chunks)),
                pltpu.SemaphoreType.DMA((chunks, 2)),
            ],
            compiler_params=pltpu.CompilerParams(
                collective_id=0, has_side_effects=True, vmem_limit_bytes=48 * 1024 * 1024
            ),
            name="lesser",
        )(pair_off, pair_count, pair_range, green, sigma, phonon)

    wide = P("energy", "slab", None, None, None, None)
    slim = P("energy", "slab", None, None, None)
    return jax.shard_map(
        body,
        mesh=mesh,
        in_specs=(wide, wide, slim, P(), P(), P()),
        out_specs=slim,
        check_vma=False,
    )
```

time: 113 us -> 57.3 us (0.51)
  Pallas kernels: 0 us -> 49.6 us
  waiting for transfers between devices: 47.1 us -> 0 us
  other arithmetic: 21.8 us -> 0 us
  matrix products: 19.4 us -> 0 us
  starting transfers between devices: 12.2 us -> 0 us
  local copies, waits for them, and re-layouts: 11.9 us -> 7.21 us
    pallas_call x0 -> x1, Pallas kernels: none -> 49.6 us  [body(): pl.pallas_call(functools.partial(kernel, slabs, energies), out_shape=jax....]
    ppermute x4 -> x0, waiting for transfers between devices: 47.1 us -> none  [the longest x1 39.2 us: extended_2(): lax.ppermute(lax.slice_in_dim(block, 0, width, axis=dim), axis, backward)]
    dot_general x24 -> x0, matrix products: 19.4 us -> none  [the longest x12 14.6 us: pair_dot(): lax.dot_general(left, right, layout, preferred_element_type=jnp.float32)]
    ppermute x4 -> x0, starting transfers between devices: 12.2 us -> none  [the longest x2 5.68 us: from_behind(): lax.ppermute(value, axis, [(source, source + steps) for source in range(l...]
    gather x3 -> x0, local copies, waits for them, and re-layouts: 8.61 us -> none  [slab_term(): chosen = jnp.take(green_row, pick, axis=0) * keep[:, None, None, None]]
    mul x3 -> x0, other arithmetic: 7.47 us -> none  [slab_term(): chosen = jnp.take(green_row, pick, axis=0) * keep[:, None, None, None]]
    unnamed x20 -> x11, local copies, waits for them, and re-layouts: 0.3 us -> 7.21 us
    and x6 -> x0, other arithmetic: 6.3 us -> none  [the longest x3 4.52 us: slab_term(): usable = (place >= 0) & (place <= 2) & (slot_ids < count)]
  transfers between devices with their start and end apart: 4 -> 0, of which waited for: 2 -> 0; matrix products, arithmetic and copies ran while one was open for 33% -> 0% of each run, Pallas kernels for 0% -> 0%
where the time goes in v1:
time: 57.3 us; the launch traced here: 56.8 us
  Pallas kernels  49.6 us (87%)
  local copies, waits for them, and re-layouts  7.21 us (13%)
    pallas_call x1, Pallas kernels, body(): pl.pallas_call(functools.partial(kernel, slabs, energies), out_shape=jax....  49.6 us
    unnamed x11, local copies, waits for them, and re-layouts  7.21 us

profile of v1, /device:TPU:130, one launch (start us, length us, event | category | flops | bytes accessed | tf_op | source)
XLA Modules:
  0.0 56.8 jit_solution(8897956053195890078)
XLA Ops:
  0.0 0.8 %copy.7.off_ref = s32[32,3]{1,0:T(8,128)S(1)} copy(s32[32,3]{0,1:T(4,128)} %param.9) | data formatting | bytes 768 | tf_op args[3]
  0.8 0.8 %copy.8.range_ref = s32[32,3]{1,0:T(8,128)S(1)} copy(s32[32,3]{0,1:T(4,128)} %param.11) | data formatting | bytes 768 | tf_op args[5]
  1.5 0.0 copy-start
  1.5 1.5 %copy-done = bf16[1,1,3,2,384,384]{5,4,3,2,1,0:T(8,128)(2,1)S(1)} copy-done((bf16[1,1,3,2,384,384]{5,4,3,2,1,0:T(8,128)(2,1)S(1)}, bf16[1,1,3,2,384,384]{5,4,3,2,1,0:T(8,128)(2,1)}, u32[]{:S(2)}) %copy-start) | copy-done | bytes 1769496
  3.0 0.0 copy-start.1
  3.0 1.5 %copy-done.1 = bf16[1,1,3,2,384,384]{5,4,3,2,1,0:T(8,128)(2,1)S(1)} copy-done((bf16[1,1,3,2,384,384]{5,4,3,2,1,0:T(8,128)(2,1)S(1)}, bf16[1,1,3,2,384,384]{5,4,3,2,1,0:T(8,128)(2,1)}, u32[]{:S(2)}) %copy-start.1) | copy-done | bytes 1769496
  4.5 0.0 copy-start.2
  4.5 1.1 %copy-done.2 = bf16[1,1,2,384,384]{4,3,2,1,0:T(8,128)(2,1)S(1)} copy-done((bf16[1,1,2,384,384]{4,3,2,1,0:T(8,128)(2,1)S(1)}, bf16[1,1,2,384,384]{4,3,2,1,0:T(8,128)(2,1)}, u32[]{:S(2)}) %copy-start.2) | copy-done | bytes 589848
  5.5 0.0 copy-start.3
  5.5 0.7 %copy-done.3 = s32[32]{0:T(128)S(1)} copy-done((s32[32]{0:T(128)S(1)}, s32[32]{0:T(128)}, u32[]{:S(2)}) %copy-start.3) | copy-done | bytes 152
  6.2 49.6 %lesser.1 = f32[1,1,2,384,384]{4,3,2,1,0:T(8,128)S(1)} custom-call(s32[32,3]{1,0:T(8,128)S(1)} %copy.7.off_ref, s32[32]{0:T(128)S(1)} %copy-done.3, s32[32,3]{1,0:T(8,128)S(1)} %copy.8.range_ref, bf16[1,1,3,2,384,384]{5,4,3,2,1,0:T(8,128)(2,1)S(1)} %copy-done, bf16[1,1,3,2,384,384]{5,4,3,2,1,0:T(8,128)(2,1)S(1)} %copy-done.1, ...), custom_call_target="tpu_custom_call" | custom-call | tf_op jit(solution)/shard_map/lesser/pallas_call | solution.py:295
  55.8 1.0 %copy.10 = f32[1,1,2,384,384]{4,3,2,1,0:T(8,128)} copy(f32[1,1,2,384,384]{4,3,2,1,0:T(8,128)S(1)} %lesser.1) | data formatting | bytes 2359296
Async XLA Ops:
  1.5 1.5 %copy-start = (bf16[1,1,3,2,384,384]{5,4,3,2,1,0:T(8,128)(2,1)S(1)}, bf16[1,1,3,2,384,384]{5,4,3,2,1,0:T(8,128)(2,1)}, u32[]{:S(2)}) copy-start(bf16[1,1,3,2,384,384]{5,4,3,2,1,0:T(8,128)(2,1)} %green_hbm.1) | copy-start | bytes 5308420
  3.0 1.5 %copy-start.1 = (bf16[1,1,3,2,384,384]{5,4,3,2,1,0:T(8,128)(2,1)S(1)}, bf16[1,1,3,2,384,384]{5,4,3,2,1,0:T(8,128)(2,1)}, u32[]{:S(2)}) copy-start(bf16[1,1,3,2,384,384]{5,4,3,2,1,0:T(8,128)(2,1)} %sigma_hbm.1) | copy-start | bytes 5308420
  4.5 1.1 %copy-start.2 = (bf16[1,1,2,384,384]{4,3,2,1,0:T(8,128)(2,1)S(1)}, bf16[1,1,2,384,384]{4,3,2,1,0:T(8,128)(2,1)}, u32[]{:S(2)}) copy-start(bf16[1,1,2,384,384]{4,3,2,1,0:T(8,128)(2,1)} %phonon_hbm.1) | copy-start | bytes 1769476
  5.5 0.7 %copy-start.3 = (s32[32]{0:T(128)S(1)}, s32[32]{0:T(128)}, u32[]{:S(2)}) copy-start(s32[32]{0:T(128)} %count_ref.1) | copy-start | bytes 388

commit v2 on v1

--- a/solution.py
+++ b/solution.py
@@ -17,13 +17,16 @@
 def kernel(
     slabs,
     energies,
+    off_hbm,
+    count_hbm,
+    range_hbm,
+    green_hbm,
+    sigma_hbm,
+    phonon_hbm,
+    out_ref,
     off_ref,
     count_ref,
     range_ref,
-    green_hbm,
-    sigma_hbm,
-    phonon_hbm,
-    out_hbm,
     green_v,
     sigma_v,
     phonon_v,
@@ -36,13 +39,11 @@
     y_v,
     part_v,
     acc_v,
-    out_v,
     local_sem,
     near_send,
     near_recv,
     send_sem,
     recv_sem,
-    out_sem,
 ):
     k = lax.axis_index("slab")
     e = lax.axis_index("energy")
@@ -52,6 +53,14 @@
     has_left, has_right = k > 0, k < slabs - 1
     has_low, has_high = e > 0, e < energies - 1
 
+    tables = [
+        pltpu.make_async_copy(source, held, local_sem.at[3 + n])
+        for n, (source, held) in enumerate(
+            ((off_hbm, off_ref), (count_hbm, count_ref), (range_hbm, range_ref))
+        )
+    ]
+    for table in tables:
+        table.start()
     load_phonon = pltpu.make_async_copy(phonon_hbm.at[0, 0], phonon_v, local_sem.at[0])
     load_sigma = pltpu.make_async_copy(sigma_hbm.at[0, 0], sigma_v, local_sem.at[1])
     load_green = pltpu.make_async_copy(green_hbm.at[0, 0], green_v, local_sem.at[2])
@@ -121,8 +130,8 @@
     def combine(place, offset, with_phonon):
         reach = []
         for q in range(slots):
-            live = (q < count_ref[k]) & (off_ref[k, q] == offset)
-            reach.append(jnp.where(live, range_ref[k, q], 0))
+            live = (q < count_ref[k]) & (off_ref[q, k] == offset)
+            reach.append(jnp.where(live, range_ref[q, k], 0))
 
         def step(t, carry):
             rows = pl.ds(pl.multiple_of(t * TILE, TILE), TILE)
@@ -150,6 +159,8 @@
             for copy in copies:
                 copy.start()
 
+    for table in tables:
+        table.wait()
     load_sigma.wait()
     combine(0, 1, False)
     start(has_right, to_right[:1])
@@ -242,7 +253,6 @@
     blocks(0, 1, 2)
     arrived(has_right, to_left[1])
     blocks(1, 1, 0)
-    writes = []
     for c in range(chunks):
         rows = slice(c * CHUNK, (c + 1) * CHUNK)
         arrived(has_left, to_right[2 + c])
@@ -256,12 +266,7 @@
                 these = slice(m * CHUNK, (m + 1) * CHUNK)
                 total = acc_v[these] + dot(a_v[c, these, 2 * CHUNK :], y_v[...])
                 for part in range(2):
-                    out_v[part, these] = total[:, part * width : (part + 1) * width]
-                    write = pltpu.make_async_copy(
-                        out_v.at[part, these], out_hbm.at[0, 0, part, these], out_sem.at[m, part]
-                    )
-                    write.start()
-                    writes.append(write)
+                    out_ref[0, 0, part, these] = total[:, part * width : (part + 1) * width]
 
     @pl.when(has_high)
     def _():
@@ -277,9 +282,6 @@
         def _():
             for copy in copies:
                 copy.wait_send()
-
-    for write in writes:
-        write.wait()
 
 
 def solution(mesh):
@@ -289,15 +291,19 @@
         width = green.shape[-1]
         slots = sigma.shape[2]
         chunks = width // CHUNK
-        smem = pl.BlockSpec(memory_space=pltpu.SMEM)
-        hbm = pl.BlockSpec(memory_space=pl.ANY)
+        hbm = pl.BlockSpec(memory_space=pltpu.HBM)
         block = (width, 2 * width)
+        operands = (pair_off.T, pair_count, pair_range.T, green, sigma, phonon)
+        operands = [pltpu.with_memory_space_constraint(v, pltpu.HBM) for v in operands]
         return pl.pallas_call(
             functools.partial(kernel, slabs, energies),
             out_shape=jax.ShapeDtypeStruct((1, 1, 2, width, width), F32),
-            in_specs=[smem, smem, smem, hbm, hbm, hbm],
-            out_specs=hbm,
+            in_specs=[hbm] * 6,
+            out_specs=pl.BlockSpec(memory_space=pltpu.VMEM),
             scratch_shapes=[
+                pltpu.SMEM((slots, slabs), jnp.int32),
+                pltpu.SMEM((slabs,), jnp.int32),
+                pltpu.SMEM((slots, slabs), jnp.int32),
                 pltpu.VMEM((3, 2, width, width), BF16),
                 pltpu.VMEM((slots, 2, width, width), BF16),
                 pltpu.VMEM((2, width, width), BF16),
@@ -310,19 +316,17 @@
                 pltpu.VMEM((4 * CHUNK, 2 * width), BF16),
                 pltpu.VMEM((2,) + block, F32),
                 pltpu.VMEM(block, F32),
-                pltpu.VMEM((2, width, width), F32),
-                pltpu.SemaphoreType.DMA((3,)),
+                pltpu.SemaphoreType.DMA((6,)),
                 pltpu.SemaphoreType.DMA((2,)),
                 pltpu.SemaphoreType.DMA((2,)),
                 pltpu.SemaphoreType.DMA((2, 2 + chunks)),
                 pltpu.SemaphoreType.DMA((2, 2 + chunks)),
-                pltpu.SemaphoreType.DMA((chunks, 2)),
             ],
             compiler_params=pltpu.CompilerParams(
                 collective_id=0, has_side_effects=True, vmem_limit_bytes=48 * 1024 * 1024
             ),
             name="lesser",
-        )(pair_off, pair_count, pair_range, green, sigma, phonon)
+        )(*operands)
 
     wide = P("energy", "slab", None, None, None, None)
     slim = P("energy", "slab", None, None, None)

time: 57.3 us -> 47.1 us (0.82)
  local copies, waits for them, and re-layouts: 7.21 us -> 1.02 us
  Pallas kernels: 49.6 us -> 45.8 us
    unnamed x11 -> x1, local copies, waits for them, and re-layouts: 7.21 us -> 1.02 us
    pallas_call x1, Pallas kernels: 49.6 us -> 45.8 us  [body(): pl.pallas_call(functools.partial(kernel, slabs, energies), out_shape=jax....]
where the time goes in v2:
time: 47.1 us; the launch traced here: 46.8 us
  Pallas kernels  45.8 us (97%)
  local copies, waits for them, and re-layouts  1.02 us (2%)
    pallas_call x1, Pallas kernels, body(): pl.pallas_call(functools.partial(kernel, slabs, energies), out_shape=jax....  45.8 us
    unnamed x1, local copies, waits for them, and re-layouts  1.02 us

profile of v2, /device:TPU:130, one launch (start us, length us, event | category | flops | bytes accessed | tf_op | source)
XLA Modules:
  0.0 46.8 jit_solution(5651477915844429509)
XLA Ops:
  0.0 45.8 %lesser.1 = f32[1,1,2,384,384]{4,3,2,1,0:T(8,128)S(1)} custom-call(s32[3,32]{1,0:T(4,128)} %bitcast.2, s32[32]{0:T(128)} %count_hbm.1, s32[3,32]{1,0:T(4,128)} %bitcast.3, bf16[1,1,3,2,384,384]{5,4,3,2,1,0:T(8,128)(2,1)} %green_hbm.1, bf16[1,1,3,2,384,384]{5,4,3,2,1,0:T(8,128)(2,1)} %sigma_hbm.1, bf16[1,1,2,384,384]{4,3,2,1,0:T(8,128)(2,1)} %phonon_hbm.1), custom_call_target="tpu_custom_call" | custom-call | tf_op jit(solution)/shard_map/lesser/pallas_call | solution.py:298
  45.8 1.0 %copy.8 = f32[1,1,2,384,384]{4,3,2,1,0:T(8,128)} copy(f32[1,1,2,384,384]{4,3,2,1,0:T(8,128)S(1)} %lesser.1) | data formatting | bytes 2359296

commit v3 on v2

v3 whole, which is shorter than its diff:
```python
import functools

import jax
import jax.numpy as jnp
from jax import lax
from jax.experimental import pallas as pl
from jax.experimental.pallas import tpu as pltpu
from jax.sharding import PartitionSpec as P

MESH = pl.DeviceIdType.MESH
F32 = jnp.float32
BF16 = jnp.bfloat16
TILE = 16
CHUNK = 128
LAST = 64


def kernel(
    slabs,
    energies,
    off_hbm,
    count_hbm,
    range_hbm,
    green_hbm,
    sigma_hbm,
    phonon_hbm,
    out_ref,
    off_ref,
    count_ref,
    range_ref,
    green_v,
    sigma_v,
    near_v,
    mine_v,
    got_v,
    b_v,
    a_v,
    side_v,
    y_v,
    part_v,
    acc_v,
    local_sem,
    near_send,
    near_recv,
    send_sem,
    recv_sem,
):
    k = lax.axis_index("slab")
    e = lax.axis_index("energy")
    width = green_v.shape[-1]
    slots = sigma_v.shape[0]
    chunks = width // CHUNK
    has_low, has_high = e > 0, e < energies - 1
    has_left, has_right = k > 0, k < slabs - 1
    goes, comes = (has_right, has_left), (has_left, has_right)

    tables = [
        pltpu.make_async_copy(source, held, local_sem.at[n])
        for n, (source, held) in enumerate(
            ((off_hbm, off_ref), (count_hbm, count_ref), (range_hbm, range_ref))
        )
    ]
    load_sigma = []
    for c in range(chunks):
        rows = slice(c * CHUNK, (c + 1) * CHUNK)
        load_sigma.append(
            pltpu.make_async_copy(
                sigma_hbm.at[0, 0, :, :, rows], sigma_v.at[:, :, rows], local_sem.at[4 + c]
            )
        )
    load_green = pltpu.make_async_copy(green_hbm.at[0, 0], green_v, local_sem.at[3])

    barrier = pltpu.get_barrier_semaphore()
    peers = (
        (has_left, {"slab": k - 1}),
        (has_right, {"slab": k + 1}),
        (has_low, {"energy": e - 1}),
        (has_high, {"energy": e + 1}),
    )
    for there, who in peers:

        @pl.when(there)
        def _():
            pl.semaphore_signal(barrier, inc=1, device_id=who, device_id_type=MESH)

    for table in tables:
        table.start()
    for load in load_sigma:
        load.start()

    def near_copy(slot, target):
        return pltpu.make_async_remote_copy(
            src_ref=phonon_hbm.at[0, 0],
            dst_ref=near_v.at[slot],
            send_sem=near_send.at[slot],
            recv_sem=near_recv.at[slot],
            device_id={"energy": target},
            device_id_type=MESH,
        )

    up, down = near_copy(0, e + 1), near_copy(1, e - 1)

    whole = slice(None)
    plan = [(0, whole, c * CHUNK, CHUNK) for c in range(chunks)]
    plan += [(1, whole, 0, width)]
    first_centre = len(plan)
    plan += [(2, whole, c * CHUNK, CHUNK) for c in range(chunks - 1)]
    plan += [(2, whole, width - CHUNK, CHUNK - LAST)]
    plan += [(2, slice(c, c + 1), width - LAST, LAST) for c in range(chunks)]
    sent = [[], []]
    for way in range(2):
        for n, (slot, these, row, count) in enumerate(plan):
            source = 4 if slot == 2 else 2 * way + slot
            sent[way].append(
                pltpu.make_async_remote_copy(
                    src_ref=mine_v.at[source, these, row : row + count],
                    dst_ref=got_v.at[way, slot, these, row : row + count],
                    send_sem=send_sem.at[way, n],
                    recv_sem=recv_sem.at[way, n],
                    device_id={"slab": (k + 1, k - 1)[way]},
                    device_id_type=MESH,
                )
            )

    def start(there, *copies):
        @pl.when(there)
        def _():
            for copy in copies:
                copy.start()

    def arrived(there, *copies):
        @pl.when(there)
        def _():
            for copy in copies:
                copy.wait_recv()

    def combine(at, offset, with_phonon, first=0, last=width // TILE):
        reach = []
        for q in range(slots):
            live = (q < count_ref[k]) & (off_ref[q, k] == offset)
            reach.append(jnp.where(live, range_ref[q, k], 0))

        def step(t, carry):
            rows = pl.ds(pl.multiple_of(t * TILE, TILE), TILE)
            col_ids = lax.broadcasted_iota(jnp.int32, (TILE, width), 1)
            inside = [col_ids < jnp.where(t * TILE < reach[q], reach[q], 0) for q in range(slots)]
            for part in range(2):
                kept = [
                    jnp.where(inside[q], sigma_v[q, part, rows, :].astype(F32), 0.0) for q in range(slots)
                ]
                total = functools.reduce(jnp.add, kept)
                if with_phonon:
                    low = near_v[0, part, rows, :].astype(F32)
                    high = near_v[1, part, rows, :].astype(F32)
                    total = total + (0.5 * (low + high)).astype(BF16).astype(F32)
                total = total.astype(BF16)
                for c in range(chunks):
                    mine_v[at, c, rows, part * CHUNK : (part + 1) * CHUNK] = total[
                        :, c * CHUNK : (c + 1) * CHUNK
                    ]
            return carry

        lax.fori_loop(first, last, step, 0)

    for table in tables:
        table.wait()
    tiles = CHUNK // TILE
    for c in range(chunks):
        load_sigma[c].wait()
        for way in range(2):
            combine(2 * way, (1, -1)[way], False, c * tiles, (c + 1) * tiles)
            if c == 0 and way == 0:
                pl.semaphore_wait(barrier, sum(there.astype(jnp.int32) for there, _ in peers))
            start(goes[way], sent[way][c])
        if c == 0:
            start(has_high, up)
            start(has_low, down)
    load_green.start()
    for way in range(2):
        combine(2 * way + 1, (2, -2)[way], False)
        start(goes[way], sent[way][chunks])

    for way in range(2):

        @pl.when(jnp.logical_not(comes[way]))
        def _():
            got_v[way] = jnp.zeros_like(got_v[way])

    for there, slot in ((has_low, 0), (has_high, 1)):

        @pl.when(jnp.logical_not(there))
        def _():
            near_v[slot] = jnp.zeros_like(near_v[slot])

    load_green.wait()
    for at in range(3):
        for part in range(2):
            flipped = green_v[at, part].astype(F32).T
            plain = flipped.astype(BF16)
            minus = (-flipped).astype(BF16)
            for c in range(chunks):
                source = slice(c * CHUNK, (c + 1) * CHUNK)
                real = slice(2 * c * CHUNK, (2 * c + 1) * CHUNK)
                imag = slice((2 * c + 1) * CHUNK, (2 * c + 2) * CHUNK)
                if part == 0:
                    b_v[at, real, :width] = plain[source]
                    b_v[at, imag, width:] = plain[source]
                else:
                    b_v[at, real, width:] = minus[source]
                    b_v[at, imag, :width] = plain[source]
    for c in range(chunks):
        for part in range(2):
            a_v[c, :, part * CHUNK : (part + 1) * CHUNK] = green_v[1, part, :, c * CHUNK : (c + 1) * CHUNK]
    for h in range(width // LAST):
        for n, at in enumerate((0, 2)):
            side_v[h, :, 2 * n * LAST : 2 * (n + 1) * LAST] = jnp.concatenate(
                [green_v[at, part, :, h * LAST : (h + 1) * LAST] for part in range(2)], axis=1
            )

    arrived(has_low, up)
    arrived(has_high, down)
    combine(4, 0, True)
    for way in range(2):
        start(goes[way], *sent[way][first_centre:])

    def dot(a, b):
        return jnp.dot(a, b, preferred_element_type=F32)

    def b_chunk(at, c):
        return b_v[at, 2 * c * CHUNK : 2 * (c + 1) * CHUNK]

    def put(at, x):
        rows = x.shape[0]
        real = x[:, :width].astype(BF16)
        imag = x[:, width:].astype(BF16)
        y_v[at : at + rows, :width] = real
        y_v[at : at + rows, width:] = imag
        y_v[at + rows : at + 2 * rows, :width] = -imag
        y_v[at + rows : at + 2 * rows, width:] = real

    for r in range(chunks):
        rows = slice(r * CHUNK, (r + 1) * CHUNK)
        x = None
        for at, partner in ((2, 0), (4, 1), (0, 2)):
            for c in range(chunks):
                term = dot(mine_v[at, c, rows], b_chunk(partner, c))
                x = term if x is None else x + term
        put(0, x)
        term = dot(a_v[r], y_v[: 2 * CHUNK])
        acc_v[...] = term if r == 0 else acc_v[...] + term

    for slot in range(2):
        for way in range(2):
            arrived(comes[way], *sent[way][chunks * slot : chunks + slot])
            partner = ((1, 2), (1, 0))[way][slot]
            for r in range(chunks):
                rows = slice(r * CHUNK, (r + 1) * CHUNK)
                x = None
                for c in range(chunks):
                    term = dot(got_v[way, slot, c, rows], b_chunk(partner, c))
                    x = term if x is None else x + term
                part_v[way, rows] = x if slot == 0 else part_v[way, rows] + x
    for n, (_, these, row, count) in enumerate(plan[first_centre:]):
        rows = slice(row, row + count)
        complete = these == whole or n == len(plan) - first_centre - 1
        for way in range(2):
            arrived(comes[way], sent[way][first_centre + n])
            x = part_v[way, rows]
            for c in range(chunks)[these]:
                x = x + dot(got_v[way, 2, c, rows], b_chunk((0, 2)[way], c))
            if complete:
                for h in range(count // LAST):
                    put(4 * h * LAST + 2 * way * LAST, x[h * LAST : (h + 1) * LAST])
            else:
                part_v[way, rows] = x
        if complete and n < len(plan) - first_centre - 1:
            total = acc_v[...]
            for h in range(count // LAST):
                total = total + dot(side_v[row // LAST + h], y_v[4 * h * LAST : 4 * (h + 1) * LAST])
            acc_v[...] = total
    for m in range(chunks):
        rows = slice(m * CHUNK, (m + 1) * CHUNK)
        total = acc_v[rows] + dot(side_v[width // LAST - 1, rows], y_v[: 4 * LAST])
        for part in range(2):
            out_ref[0, 0, part, rows] = total[:, part * width : (part + 1) * width]

    for there, copies in ((has_high, [up]), (has_low, [down]), (has_right, sent[0]), (has_left, sent[1])):

        @pl.when(there)
        def _():
            for copy in copies:
                copy.wait_send()


def solution(mesh):
    slabs, energies = mesh.shape["slab"], mesh.shape["energy"]

    def body(green, sigma, phonon, pair_off, pair_count, pair_range):
        width = green.shape[-1]
        slots = sigma.shape[2]
        chunks = width // CHUNK
        copies = 2 * chunks + 1 + chunks
        hbm = pl.BlockSpec(memory_space=pltpu.HBM)
        split = (chunks, width, 2 * CHUNK)
        operands = (pair_off.T, pair_count, pair_range.T, green, sigma, phonon)
        operands = [pltpu.with_memory_space_constraint(v, pltpu.HBM) for v in operands]
        return pl.pallas_call(
            functools.partial(kernel, slabs, energies),
            out_shape=jax.ShapeDtypeStruct((1, 1, 2, width, width), F32),
            in_specs=[hbm] * 6,
            out_specs=pl.BlockSpec(memory_space=pltpu.VMEM),
            scratch_shapes=[
                pltpu.SMEM((slots, slabs), jnp.int32),
                pltpu.SMEM((slabs,), jnp.int32),
                pltpu.SMEM((slots, slabs), jnp.int32),
                pltpu.VMEM((3, 2, width, width), BF16),
                pltpu.VMEM((slots, 2, width, width), BF16),
                pltpu.VMEM((2, 2, width, width), BF16),
                pltpu.VMEM((5,) + split, BF16),
                pltpu.VMEM((2, 3) + split, BF16),
                pltpu.VMEM((3, 2 * width, 2 * width), BF16),
                pltpu.VMEM(split, BF16),
                pltpu.VMEM((width // LAST, width, 4 * LAST), BF16),
                pltpu.VMEM((4 * CHUNK, 2 * width), BF16),
                pltpu.VMEM((2, width, 2 * width), F32),
                pltpu.VMEM((width, 2 * width), F32),
                pltpu.SemaphoreType.DMA((4 + chunks,)),
                pltpu.SemaphoreType.DMA((2,)),
                pltpu.SemaphoreType.DMA((2,)),
                pltpu.SemaphoreType.DMA((2, copies)),
                pltpu.SemaphoreType.DMA((2, copies)),
            ],
            compiler_params=pltpu.CompilerParams(
                collective_id=0, has_side_effects=True, vmem_limit_bytes=48 * 1024 * 1024
            ),
            name="lesser",
        )(*operands)

    wide = P("energy", "slab", None, None, None, None)
    slim = P("energy", "slab", None, None, None)
    return jax.shard_map(
        body,
        mesh=mesh,
        in_specs=(wide, wide, slim, P(), P(), P()),
        out_specs=slim,
        check_vma=False,
    )
```

time: 47.1 us -> 46.9 us (level)
  no operation moved by 1% of the time
where the time goes in v3:
time: 46.9 us; the launch traced here: 46.8 us
  Pallas kernels  45.8 us (98%)
  local copies, waits for them, and re-layouts  1.02 us (2%)
    pallas_call x1, Pallas kernels, body(): pl.pallas_call(functools.partial(kernel, slabs, energies), out_shape=jax....  45.8 us
    unnamed x1, local copies, waits for them, and re-layouts  1.02 us

profile of v3, /device:TPU:130, one launch (start us, length us, event | category | flops | bytes accessed | tf_op | source)
XLA Modules:
  0.0 46.8 jit_solution(15652064250455592104)
XLA Ops:
  0.0 45.8 %lesser.1 = f32[1,1,2,384,384]{4,3,2,1,0:T(8,128)S(1)} custom-call(s32[3,32]{1,0:T(4,128)} %bitcast.2, s32[32]{0:T(128)} %count_hbm.1, s32[3,32]{1,0:T(4,128)} %bitcast.3, bf16[1,1,3,2,384,384]{5,4,3,2,1,0:T(8,128)(2,1)} %green_hbm.1, bf16[1,1,3,2,384,384]{5,4,3,2,1,0:T(8,128)(2,1)} %sigma_hbm.1, bf16[1,1,2,384,384]{4,3,2,1,0:T(8,128)(2,1)} %phonon_hbm.1), custom_call_target="tpu_custom_call" | custom-call | tf_op jit(solution)/shard_map/lesser/pallas_call | solution.py:307
  45.8 1.0 %copy.8 = f32[1,1,2,384,384]{4,3,2,1,0:T(8,128)} copy(f32[1,1,2,384,384]{4,3,2,1,0:T(8,128)S(1)} %lesser.1) | data formatting | bytes 2359296

commit v4 on v3

v4 whole, which is shorter than its diff:
```python
import functools

import jax
import jax.numpy as jnp
from jax import lax
from jax.experimental import pallas as pl
from jax.experimental.pallas import tpu as pltpu
from jax.sharding import PartitionSpec as P

MESH = pl.DeviceIdType.MESH
F32 = jnp.float32
BF16 = jnp.bfloat16
TILE = 16
CHUNK = 128
LAST = 64
UNIT = 96
GROUP = 3
LIST = 24
DIRECT = 18
SHARED = 12
HOP = 4
OFFSETS = (1, 2, -1, -2)


def extent(reach):
    steps = [(reach >= n * UNIT).astype(jnp.int32) for n in range(1, 5)]
    down = steps[0] + steps[1] + steps[2] + steps[3]
    across = steps[0] + steps[1] + steps[2]
    return down, across, down * across


def turned(slab, way):
    place = lax.rem(slab, HOP)
    paired = jnp.where(lax.rem(lax.div(slab, HOP), 2) == 0, HOP, -HOP)
    if way == 0:
        return jnp.where(place == HOP - 1, -HOP, jnp.where(place == 1, paired, HOP))
    return jnp.where(place == 0, HOP, jnp.where(place == 2, paired, -HOP))


def detours(slab, way, slabs):
    low, high = (0, slabs - 2) if way == 0 else (1, slabs - 1)
    relay = slab + turned(slab, way)
    return (slab >= low) & (slab <= high) & (relay >= low) & (relay <= high)


def relayed(relay, way):
    turn = turned(relay, way)
    return relay + jnp.where(lax.rem(relay, HOP) == 1 + way, turn, -turn)


def crowded_kernel(off_ref, count_ref, range_ref, out_ref):
    off, reach = off_ref[...], range_ref[...]
    slots, slabs = off.shape
    live = lax.broadcasted_iota(jnp.int32, off.shape, 0) < count_ref[...]
    slab = lax.broadcasted_iota(jnp.int32, (1, slabs), 1)
    crowded = jnp.zeros((1, slabs), F32)
    for way in range(2):
        filled = jnp.zeros((1, slabs), jnp.int32)
        for offset in OFFSETS[2 * way : 2 * way + 2]:
            widest = jnp.max(jnp.where(live & (off == offset), reach, 0), axis=0, keepdims=True)
            filled = filled + extent(widest)[2]
        above = jnp.concatenate([filled[:, HOP:], filled[:, :HOP]], axis=1)
        below = jnp.concatenate([filled[:, -HOP:], filled[:, :-HOP]], axis=1)
        relay = jnp.where(turned(slab, way) > 0, above, below)
        stuck = (relay > SHARED) | jnp.logical_not(detours(slab, way, slabs))
        crowded = crowded + ((filled > DIRECT) & stuck).astype(F32)
    out_ref[0] = jnp.max(crowded).astype(jnp.int32)


def dot(a, b):
    return jnp.dot(a, b, preferred_element_type=F32)


def start(there, *copies):
    @pl.when(there)
    def _():
        for copy in copies:
            copy.start()


def arrived(there, *copies):
    @pl.when(there)
    def _():
        for copy in copies:
            copy.wait_recv()


def gone(there, *copies):
    @pl.when(there)
    def _():
        for copy in copies:
            copy.wait_send()


def greet(peers):
    barrier = pltpu.get_barrier_semaphore()
    for there, who in peers:

        @pl.when(there)
        def _():
            pl.semaphore_signal(barrier, inc=1, device_id=who, device_id_type=MESH)


def greeted(peers):
    barrier = pltpu.get_barrier_semaphore()
    pl.semaphore_wait(barrier, sum(there.astype(jnp.int32) for there, _ in peers))


def prepare(green_v, b_v, a_v, side_v):
    width = green_v.shape[-1]
    for at in range(3):
        for part in range(2):
            flipped = green_v[at, part].astype(F32).T
            plain = flipped.astype(BF16)
            minus = (-flipped).astype(BF16)
            for c in range(width // CHUNK):
                source = slice(c * CHUNK, (c + 1) * CHUNK)
                real = slice(2 * c * CHUNK, (2 * c + 1) * CHUNK)
                imag = slice((2 * c + 1) * CHUNK, (2 * c + 2) * CHUNK)
                if part == 0:
                    b_v[at, real, :width] = plain[source]
                    b_v[at, imag, width:] = plain[source]
                else:
                    b_v[at, real, width:] = minus[source]
                    b_v[at, imag, :width] = plain[source]
    for c in range(width // CHUNK):
        for part in range(2):
            a_v[c, :, part * CHUNK : (part + 1) * CHUNK] = green_v[1, part, :, c * CHUNK : (c + 1) * CHUNK]
    for h in range(width // LAST):
        for n, at in enumerate((0, 2)):
            side_v[h, :, 2 * n * LAST : 2 * (n + 1) * LAST] = jnp.concatenate(
                [green_v[at, part, :, h * LAST : (h + 1) * LAST] for part in range(2)], axis=1
            )


def b_chunk(b_v, at, c):
    return b_v[at, 2 * c * CHUNK : 2 * (c + 1) * CHUNK]


def put(y_v, at, x):
    rows, width = x.shape[0], x.shape[1] // 2
    real = x[:, :width].astype(BF16)
    imag = x[:, width:].astype(BF16)
    y_v[at : at + rows, :width] = real
    y_v[at : at + rows, width:] = imag
    y_v[at + rows : at + 2 * rows, :width] = -imag
    y_v[at + rows : at + 2 * rows, width:] = real


def centre_plan(width):
    chunks, whole = width // CHUNK, slice(None)
    plan = [(whole, c * CHUNK, CHUNK) for c in range(chunks - 1)]
    plan += [(whole, width - CHUNK, CHUNK - LAST)]
    return plan + [(slice(c, c + 1), width - LAST, LAST) for c in range(chunks)]


def finish(centre, comes, cent, b_v, side_v, y_v, part_v, acc_v, out_ref):
    width = acc_v.shape[0]
    chunks = width // CHUNK
    plan = centre_plan(width)
    for n, (these, row, count) in enumerate(plan):
        rows = slice(row, row + count)
        final = n == len(plan) - 1
        complete = these == slice(None) or final
        for way in range(2):
            arrived(comes[way], centre[way][n])
            x = part_v[way, rows]
            for c in range(chunks)[these]:
                x = x + dot(cent(way, c, rows), b_chunk(b_v, (0, 2)[way], c))
            if complete:
                for h in range(count // LAST):
                    put(y_v, 4 * h * LAST + 2 * way * LAST, x[h * LAST : (h + 1) * LAST])
            else:
                part_v[way, rows] = x
        if complete and not final:
            total = acc_v[...]
            for h in range(count // LAST):
                total = total + dot(side_v[row // LAST + h], y_v[4 * h * LAST : 4 * (h + 1) * LAST])
            acc_v[...] = total
    for m in range(chunks):
        rows = slice(m * CHUNK, (m + 1) * CHUNK)
        total = acc_v[rows] + dot(side_v[width // LAST - 1, rows], y_v[: 4 * LAST])
        for part in range(2):
            out_ref[0, 0, part, rows] = total[:, part * width : (part + 1) * width]


def straight_kernel(
    slabs,
    energies,
    off_hbm,
    count_hbm,
    range_hbm,
    green_hbm,
    sigma_hbm,
    phonon_hbm,
    out_ref,
    off_ref,
    count_ref,
    range_ref,
    green_v,
    sigma_v,
    near_v,
    mine_v,
    got_v,
    b_v,
    a_v,
    side_v,
    y_v,
    part_v,
    acc_v,
    local_sem,
    near_send,
    near_recv,
    send_sem,
    recv_sem,
):
    k = lax.axis_index("slab")
    e = lax.axis_index("energy")
    width = green_v.shape[-1]
    slots = sigma_v.shape[0]
    chunks = width // CHUNK
    has_low, has_high = e > 0, e < energies - 1
    has_left, has_right = k > 0, k < slabs - 1
    goes, comes = (has_right, has_left), (has_left, has_right)

    tables = [
        pltpu.make_async_copy(source, held, local_sem.at[n])
        for n, (source, held) in enumerate(
            ((off_hbm, off_ref), (count_hbm, count_ref), (range_hbm, range_ref))
        )
    ]
    load_sigma = []
    for c in range(chunks):
        rows = slice(c * CHUNK, (c + 1) * CHUNK)
        load_sigma.append(
            pltpu.make_async_copy(
                sigma_hbm.at[0, 0, :, :, rows], sigma_v.at[:, :, rows], local_sem.at[4 + c]
            )
        )
    load_green = pltpu.make_async_copy(green_hbm.at[0, 0], green_v, local_sem.at[3])

    peers = (
        (has_left, {"slab": k - 1}),
        (has_right, {"slab": k + 1}),
        (has_low, {"energy": e - 1}),
        (has_high, {"energy": e + 1}),
    )
    greet(peers)
    for table in tables:
        table.start()
    for load in load_sigma:
        load.start()

    def near_copy(slot, target):
        return pltpu.make_async_remote_copy(
            src_ref=phonon_hbm.at[0, 0],
            dst_ref=near_v.at[slot],
            send_sem=near_send.at[slot],
            recv_sem=near_recv.at[slot],
            device_id={"energy": target},
            device_id_type=MESH,
        )

    up, down = near_copy(0, e + 1), near_copy(1, e - 1)

    whole = slice(None)
    plan = [(0, whole, c * CHUNK, CHUNK) for c in range(chunks)]
    plan += [(1, whole, 0, width)]
    first_centre = len(plan)
    plan += [(2,) + piece for piece in centre_plan(width)]
    sent = [[], []]
    for way in range(2):
        for n, (slot, these, row, count) in enumerate(plan):
            source = 4 if slot == 2 else 2 * way + slot
            sent[way].append(
                pltpu.make_async_remote_copy(
                    src_ref=mine_v.at[source, these, row : row + count],
                    dst_ref=got_v.at[way, slot, these, row : row + count],
                    send_sem=send_sem.at[way, n],
                    recv_sem=recv_sem.at[way, n],
                    device_id={"slab": (k + 1, k - 1)[way]},
                    device_id_type=MESH,
                )
            )

    def combine(at, offset, with_phonon, first=0, last=width // TILE):
        reach = []
        for q in range(slots):
            live = (q < count_ref[k]) & (off_ref[q, k] == offset)
            reach.append(jnp.where(live, range_ref[q, k], 0))

        def step(t, carry):
            rows = pl.ds(pl.multiple_of(t * TILE, TILE), TILE)
            col_ids = lax.broadcasted_iota(jnp.int32, (TILE, width), 1)
            inside = [col_ids < jnp.where(t * TILE < reach[q], reach[q], 0) for q in range(slots)]
            for part in range(2):
                kept = [
                    jnp.where(inside[q], sigma_v[q, part, rows, :].astype(F32), 0.0) for q in range(slots)
                ]
                total = functools.reduce(jnp.add, kept)
                if with_phonon:
                    low = near_v[0, part, rows, :].astype(F32)
                    high = near_v[1, part, rows, :].astype(F32)
                    total = total + (0.5 * (low + high)).astype(BF16).astype(F32)
                total = total.astype(BF16)
                for c in range(chunks):
                    mine_v[at, c, rows, part * CHUNK : (part + 1) * CHUNK] = total[
                        :, c * CHUNK : (c + 1) * CHUNK
                    ]
            return carry

        lax.fori_loop(first, last, step, 0)

    for table in tables:
        table.wait()
    tiles = CHUNK // TILE
    for c in range(chunks):
        load_sigma[c].wait()
        for way in range(2):
            combine(2 * way, (1, -1)[way], False, c * tiles, (c + 1) * tiles)
            if c == 0 and way == 0:
                greeted(peers)
            start(goes[way], sent[way][c])
        if c == 0:
            start(has_high, up)
            start(has_low, down)
    load_green.start()
    for way in range(2):
        combine(2 * way + 1, (2, -2)[way], False)
        start(goes[way], sent[way][chunks])

    for way in range(2):

        @pl.when(jnp.logical_not(comes[way]))
        def _():
            got_v[way] = jnp.zeros_like(got_v[way])

    for there, slot in ((has_low, 0), (has_high, 1)):

        @pl.when(jnp.logical_not(there))
        def _():
            near_v[slot] = jnp.zeros_like(near_v[slot])

    load_green.wait()
    prepare(green_v, b_v, a_v, side_v)

    arrived(has_low, up)
    arrived(has_high, down)
    combine(4, 0, True)
    for way in range(2):
        start(goes[way], *sent[way][first_centre:])

    for r in range(chunks):
        rows = slice(r * CHUNK, (r + 1) * CHUNK)
        x = None
        for at, partner in ((2, 0), (4, 1), (0, 2)):
            for c in range(chunks):
                term = dot(mine_v[at, c, rows], b_chunk(b_v, partner, c))
                x = term if x is None else x + term
        put(y_v, 0, x)
        term = dot(a_v[r], y_v[: 2 * CHUNK])
        acc_v[...] = term if r == 0 else acc_v[...] + term

    for slot in range(2):
        for way in range(2):
            arrived(comes[way], *sent[way][chunks * slot : chunks + slot])
            partner = ((1, 2), (1, 0))[way][slot]
            for r in range(chunks):
                rows = slice(r * CHUNK, (r + 1) * CHUNK)
                x = None
                for c in range(chunks):
                    term = dot(got_v[way, slot, c, rows], b_chunk(b_v, partner, c))
                    x = term if x is None else x + term
                part_v[way, rows] = x if slot == 0 else part_v[way, rows] + x
    centre = [copies[first_centre:] for copies in sent]
    finish(
        centre, comes, lambda way, c, rows: got_v[way, 2, c, rows], b_v, side_v, y_v, part_v, acc_v, out_ref
    )

    gone(has_high, up)
    gone(has_low, down)
    gone(has_right, *sent[0])
    gone(has_left, *sent[1])


def around_kernel(
    slabs,
    energies,
    off_hbm,
    count_hbm,
    range_hbm,
    green_hbm,
    sigma_hbm,
    phonon_hbm,
    out_ref,
    off_ref,
    count_ref,
    range_ref,
    green_v,
    sigma_v,
    near_v,
    mine_v,
    own_v,
    list_v,
    from_left_v,
    from_right_v,
    back_left_v,
    back_right_v,
    spill_v,
    cent_v,
    block_v,
    b_v,
    a_v,
    side_v,
    y_v,
    part_v,
    acc_v,
    local_sem,
    near_send,
    near_recv,
    unit_send,
    unit_recv,
    spill_send,
    spill_recv,
    back_send,
    back_recv,
    cent_send,
    cent_recv,
):
    k = lax.axis_index("slab")
    e = lax.axis_index("energy")
    width = green_v.shape[-1]
    slots = sigma_v.shape[0]
    chunks = width // CHUNK
    has_low, has_high = e > 0, e < energies - 1

    has_left, has_right = k > 0, k < slabs - 1

    tables = [
        pltpu.make_async_copy(source, held, local_sem.at[n])
        for n, (source, held) in enumerate(
            ((off_hbm, off_ref), (count_hbm, count_ref), (range_hbm, range_ref))
        )
    ]
    load_sigma = []
    for c in range(chunks):
        rows = slice(c * CHUNK, (c + 1) * CHUNK)
        load_sigma.append(
            pltpu.make_async_copy(
                sigma_hbm.at[0, 0, :, :, rows], sigma_v.at[:, :, rows], local_sem.at[4 + c]
            )
        )
    load_green = pltpu.make_async_copy(green_hbm.at[0, 0], green_v, local_sem.at[3])
    peers = (
        (has_left, {"slab": k - 1}),
        (has_right, {"slab": k + 1}),
        (has_low, {"energy": e - 1}),
        (has_high, {"energy": e + 1}),
        (k >= HOP, {"slab": k - HOP}),
        (k < slabs - HOP, {"slab": k + HOP}),
    )
    greet(peers)
    for table in tables:
        table.start()
    for load in load_sigma:
        load.start()

    def near_copy(slot, target):
        return pltpu.make_async_remote_copy(
            src_ref=phonon_hbm.at[0, 0],
            dst_ref=near_v.at[slot],
            send_sem=near_send.at[slot],
            recv_sem=near_recv.at[slot],
            device_id={"energy": target},
            device_id_type=MESH,
        )

    up, down = near_copy(0, e + 1), near_copy(1, e - 1)

    def remote(source, target, sent, received, slab):
        return pltpu.make_async_remote_copy(
            src_ref=source,
            dst_ref=target,
            send_sem=sent,
            recv_sem=received,
            device_id={"slab": slab},
            device_id_type=MESH,
        )

    sends = [detours(k, way, slabs) for way in range(2)]
    rides = [relayed(k, way) for way in range(2)]
    relays = [detours(rides[way], way, slabs) for way in range(2)]
    handed = [relayed(k + step, way) for way, step in ((0, -1), (1, 1))]
    hands = [there & detours(handed[way], way, slabs) for way, there in enumerate((has_left, has_right))]
    gets = [there & detours(k + step, way, slabs) for way, (there, step) in enumerate(((has_left, -1), (has_right, 1)))]
    beside = (k + 1, k - 1)
    goes, comes = (has_right, has_left), (has_left, has_right)
    got_v, back_v = (from_left_v, from_right_v), (back_left_v, back_right_v)
    units = (slice(0, 9), slice(12, 15), slice(9, 12), slice(15, 18))
    halves = (slice(0, GROUP), slice(GROUP, 2 * GROUP))
    direct, spill, returned, centre = [[], []], [[], []], [[], []], [[], []]
    for way in range(2):
        for n, these in enumerate(units):
            direct[way].append(
                remote(
                    list_v.at[way, these],
                    got_v[way].at[these],
                    unit_send.at[way, n],
                    unit_recv.at[way, n],
                    beside[way],
                )
            )
        for h, these in enumerate(halves):
            spill[way].append(
                remote(
                    list_v.at[way, DIRECT + h * GROUP : DIRECT + (h + 1) * GROUP],
                    spill_v.at[way, these],
                    spill_send.at[way, h],
                    spill_recv.at[way, h],
                    k + turned(k, way),
                )
            )
            returned[way].append(
                remote(
                    got_v[way].at[SHARED + h * GROUP : SHARED + (h + 1) * GROUP],
                    back_v[way].at[these],
                    back_send.at[way, h],
                    back_recv.at[way, h],
                    handed[way] + (1, -1)[way],
                )
            )
        for n, (these, row, count) in enumerate(centre_plan(width)):
            centre[way].append(
                remote(
                    own_v.at[these, row : row + count],
                    cent_v.at[way, these, row : row + count],
                    cent_send.at[way, n],
                    cent_recv.at[way, n],
                    beside[way],
                )
            )

    def live_reach(slab, q, offset):
        live = (q < count_ref[slab]) & (off_ref[q, slab] == offset)
        return jnp.where(live, range_ref[q, slab], 0)

    def combine(wanted, with_phonon, first=0, last=width // TILE):
        reach = [[live_reach(k, q, offset) for q in range(slots)] for _, offset in wanted]

        def step(t, carry):
            rows = pl.ds(pl.multiple_of(t * TILE, TILE), TILE)
            col_ids = lax.broadcasted_iota(jnp.int32, (TILE, width), 1)
            m = lax.div(t, UNIT // TILE)
            unit_rows = pl.ds(pl.multiple_of(t * TILE - m * UNIT, TILE), TILE)
            inside = [
                [col_ids < jnp.where(t * TILE < reach[n][q], reach[n][q], 0) for q in range(slots)]
                for n in range(len(wanted))
            ]
            for part in range(2):
                terms = [sigma_v[q, part, rows, :].astype(F32) for q in range(slots)]
                for n, (at, _) in enumerate(wanted):
                    kept = [jnp.where(inside[n][q], terms[q], 0.0) for q in range(slots)]
                    total = functools.reduce(jnp.add, kept)
                    if with_phonon:
                        low = near_v[0, part, rows, :].astype(F32)
                        high = near_v[1, part, rows, :].astype(F32)
                        total = total + (0.5 * (low + high)).astype(BF16).astype(F32)
                    total = total.astype(BF16)
                    lanes = slice(part * CHUNK, (part + 1) * CHUNK)
                    for c in range(chunks):
                        value = total[:, c * CHUNK : (c + 1) * CHUNK]
                        if with_phonon:
                            own_v[c, rows, lanes] = value
                        else:
                            mine_v[at, m, c, unit_rows, lanes] = value
            return carry

        lax.fori_loop(first, last, step, 0)

    def layout(slab, way):
        blocks = []
        for offset in OFFSETS[2 * way : 2 * way + 2]:
            reach = functools.reduce(jnp.maximum, [live_reach(slab, q, offset) for q in range(slots)])
            blocks.append(extent(reach))
        return blocks

    def pack(way, first, last):
        (_, across_a, size_a), (_, across_b, size_b) = layout(k, way)

        def step(p, carry):
            in_a = p < size_a
            unit = jnp.where(in_a, p, jnp.maximum(p - size_a, 0))
            across = jnp.where(in_a, across_a, across_b)
            row = jnp.where(across == 3, lax.div(unit, 3), jnp.where(across == 2, lax.div(unit, 2), unit))
            col = jnp.clip(unit - row * across, 0, chunks - 1)
            row = jnp.clip(row, 0, width // UNIT - 1)
            at = 2 * way + jnp.where(in_a, 0, 1)
            keep = jnp.where(p < size_a + size_b, 1.0, 0.0).astype(BF16)
            list_v[way, p] = mine_v[at, row, col] * keep
            return carry

        lax.fori_loop(first, last, step, 0)

    for table in tables:
        table.wait()
    tiles = width // TILE // chunks
    for way in range(2):
        wanted = [(2 * way + n, OFFSETS[2 * way + n]) for n in range(2)]
        if way == 0:
            for c in range(chunks):
                load_sigma[c].wait()
                combine(wanted, False, c * tiles, (c + 1) * tiles)
            load_green.start()
        else:
            combine(wanted, False)
        pack(way, 0, LIST)
        if way == 0:
            greeted(peers)
        start(sends[way], spill[way][0])
        start(goes[way], direct[way][0])
        if way == 0:
            start(has_high, up)
            start(has_low, down)
    for way in range(2):
        start(sends[way], spill[way][1])

    for way in range(2):

        @pl.when(jnp.logical_not(comes[way]))
        def _():
            got_v[way][...] = jnp.zeros_like(got_v[way])
            cent_v[way] = jnp.zeros_like(cent_v[way])

        @pl.when(jnp.logical_not(gets[way]))
        def _():
            back_v[way][...] = jnp.zeros_like(back_v[way])

        @pl.when(jnp.logical_not(relays[way]))
        def _():
            spill_v[way] = jnp.zeros_like(spill_v[way])

    for there, slot in ((has_low, 0), (has_high, 1)):

        @pl.when(jnp.logical_not(there))
        def _():
            near_v[slot] = jnp.zeros_like(near_v[slot])

    load_green.wait()
    prepare(green_v, b_v, a_v, side_v)

    arrived(has_low, up)
    arrived(has_high, down)
    combine([(4, 0)], True)

    def merge(h):
        for way in range(2):
            arrived(relays[way], spill[way][h])
            for j in range(h * GROUP, (h + 1) * GROUP):
                list_v[way, SHARED + j] = list_v[way, SHARED + j] + spill_v[way, j]

    merge(0)
    for way in range(2):
        start(goes[way], direct[way][1], direct[way][2])

    for n, (at, partner) in enumerate(((2, 0), (0, 2))):
        for r in range(2):
            rows = slice(r * width // 2, (r + 1) * width // 2)
            these = slice(rows.start // UNIT, rows.stop // UNIT)
            x = None
            for c in range(chunks):
                term = dot(mine_v[at, these, c].reshape(width // 2, 2 * CHUNK), b_chunk(b_v, partner, c))
                x = term if x is None else x + term
            part_v[0, rows] = x if n == 0 else part_v[0, rows] + x
    for r in range(chunks):
        rows = slice(r * CHUNK, (r + 1) * CHUNK)
        x = part_v[0, rows]
        for c in range(chunks):
            x = x + dot(own_v[c, rows], b_chunk(b_v, 1, c))
        put(y_v, 0, x)
        term = dot(a_v[r], y_v[: 2 * CHUNK])
        acc_v[...] = term if r == 0 else acc_v[...] + term

    merge(1)
    for way in range(2):
        start(goes[way], direct[way][3], *centre[way])
    for n, h in ((1, 0), (3, 1)):
        for way in range(2):
            arrived(comes[way], direct[way][n])
            start(hands[way], returned[way][h])

    def multiply(way, source, first, last, down_n, across_n, before, partner, fresh):
        for m in range(width // UNIT):
            for c in range(chunks):
                position = before + m * across_n + c
                there = (m < down_n) & (c < across_n) & (position >= first) & (position < last)
                keep = jnp.where(there, 1.0, 0.0).astype(BF16)
                position = jnp.clip(position - first, 0, last - first - 1)
                block_v[c, m * UNIT : (m + 1) * UNIT] = source[position] * keep
        for r in range(chunks):
            rows = slice(r * CHUNK, (r + 1) * CHUNK)
            x = None
            for c in range(chunks):
                term = dot(block_v[c, rows], b_chunk(b_v, partner, c))
                x = term if x is None else x + term
            part_v[way, rows] = x if fresh else part_v[way, rows] + x

    blocks = [
        layout(jnp.maximum(k - 1, 0), 0),
        layout(jnp.minimum(k + 1, slabs - 1), 1),
    ]
    for way in range(2):
        (down_a, across_a, size_a), (down_b, across_b, _) = blocks[way]
        partner_a, partner_b = ((1, 2), (1, 0))[way]
        arrived(comes[way], direct[way][0], direct[way][2])
        multiply(way, got_v[way], 0, DIRECT, down_a, across_a, 0, partner_a, True)
        multiply(way, got_v[way], 0, DIRECT, down_b, across_b, size_a, partner_b, False)
    for way in range(2):
        (_, _, size_a), (down_b, across_b, _) = blocks[way]
        partner_b = (2, 0)[way]
        arrived(gets[way], *returned[way])
        multiply(way, back_v[way], DIRECT, LIST, down_b, across_b, size_a, partner_b, False)

    finish(
        centre, comes, lambda way, c, rows: cent_v[way, c, rows], b_v, side_v, y_v, part_v, acc_v, out_ref
    )

    gone(has_high, up)
    gone(has_low, down)
    for way in range(2):
        gone(goes[way], *direct[way], *centre[way])
        gone(sends[way], *spill[way])
        gone(hands[way], *returned[way])


def solution(mesh):
    slabs, energies = mesh.shape["slab"], mesh.shape["energy"]

    def body(green, sigma, phonon, pair_off, pair_count, pair_range):
        width = green.shape[-1]
        slots = sigma.shape[2]
        chunks = width // CHUNK
        pieces = len(centre_plan(width))
        hbm = pl.BlockSpec(memory_space=pltpu.HBM)
        vmem = pl.BlockSpec(memory_space=pltpu.VMEM)
        split = (chunks, width, 2 * CHUNK)
        unit = (UNIT, 2 * CHUNK)
        operands = (pair_off.T, pair_count, pair_range.T, green, sigma, phonon)
        operands = [pltpu.with_memory_space_constraint(v, pltpu.HBM) for v in operands]
        taken = [
            pltpu.SMEM((slots, slabs), jnp.int32),
            pltpu.SMEM((slabs,), jnp.int32),
            pltpu.SMEM((slots, slabs), jnp.int32),
            pltpu.VMEM((3, 2, width, width), BF16),
            pltpu.VMEM((slots, 2, width, width), BF16),
            pltpu.VMEM((2, 2, width, width), BF16),
        ]
        factors = [
            pltpu.VMEM((3, 2 * width, 2 * width), BF16),
            pltpu.VMEM(split, BF16),
            pltpu.VMEM((width // LAST, width, 4 * LAST), BF16),
            pltpu.VMEM((4 * CHUNK, 2 * width), BF16),
            pltpu.VMEM((2, width, 2 * width), F32),
            pltpu.VMEM((width, 2 * width), F32),
            pltpu.SemaphoreType.DMA((4 + chunks,)),
            pltpu.SemaphoreType.DMA((2,)),
            pltpu.SemaphoreType.DMA((2,)),
        ]

        def flags(count):
            return [pltpu.SemaphoreType.DMA((2, count))] * 2

        def call(what, number, name, blocks, semaphores, *operands):
            return pl.pallas_call(
                functools.partial(what, slabs, energies),
                out_shape=jax.ShapeDtypeStruct((1, 1, 2, width, width), F32),
                in_specs=[hbm] * 6,
                out_specs=vmem,
                scratch_shapes=taken + blocks + factors + semaphores,
                compiler_params=pltpu.CompilerParams(
                    collective_id=number, has_side_effects=True, vmem_limit_bytes=48 * 1024 * 1024
                ),
                name=name,
            )(*operands)

        straight = functools.partial(
            call,
            straight_kernel,
            0,
            "straight",
            [pltpu.VMEM((5,) + split, BF16), pltpu.VMEM((2, 3) + split, BF16)],
            flags(chunks + 1 + pieces),
        )
        around = functools.partial(
            call,
            around_kernel,
            1,
            "around",
            [
                pltpu.VMEM((4, width // UNIT, chunks) + unit, BF16),
                pltpu.VMEM(split, BF16),
                pltpu.VMEM((2, LIST) + unit, BF16),
                pltpu.VMEM((DIRECT,) + unit, BF16),
                pltpu.VMEM((DIRECT,) + unit, BF16),
                pltpu.VMEM((LIST - DIRECT,) + unit, BF16),
                pltpu.VMEM((LIST - DIRECT,) + unit, BF16),
                pltpu.VMEM((2, LIST - DIRECT) + unit, BF16),
                pltpu.VMEM((2,) + split, BF16),
                pltpu.VMEM(split, BF16),
            ],
            flags(4) + flags(2) + flags(2) + flags(pieces),
        )
        crowded = pl.pallas_call(
            crowded_kernel,
            out_shape=jax.ShapeDtypeStruct((1,), jnp.int32),
            in_specs=[vmem] * 3,
            out_specs=pl.BlockSpec(memory_space=pltpu.SMEM),
            name="crowded",
        )(pair_off.T, pair_count[None], pair_range.T)
        return lax.cond(crowded[0] > 0, straight, around, *operands)

    wide = P("energy", "slab", None, None, None, None)
    slim = P("energy", "slab", None, None, None)
    return jax.shard_map(
        body,
        mesh=mesh,
        in_specs=(wide, wide, slim, P(), P(), P()),
        out_specs=slim,
        check_vma=False,
    )
```

time: 46.9 us -> 45.3 us (0.966); the launches traced: 46.8 us -> 44.4 us
  Pallas kernels: 45.8 us -> 42.5 us
  between operations: 0.01 us -> 0.67 us
    pallas_call x1 -> x2, Pallas kernels: 45.8 us -> 42.5 us  [the longest x1 41.1 us: call(): pl.pallas_call(functools.partial(what, slabs, energies), out_shape=jax.Sh...]
where the time goes in v4:
time: 45.3 us; the launch traced here: 44.4 us
  Pallas kernels  42.5 us (94%)
  local copies, waits for them, and re-layouts  1.02 us (2%)
  between operations  0.67 us (1%)
    pallas_call x1, Pallas kernels, call(): pl.pallas_call(functools.partial(what, slabs, energies), out_shape=jax.Sh...  41.1 us
    pallas_call x1, Pallas kernels, body(): pl.pallas_call(crowded_kernel, out_shape=jax.ShapeDtypeStruct((1,), jnp.i...  1.44 us
    unnamed x1, local copies, waits for them, and re-layouts  1.02 us

profile of v4, /device:TPU:130, one launch (start us, length us, event | category | flops | bytes accessed | tf_op | source)
XLA Modules:
  0.0 44.4 jit_solution(4830477997948139711)
XLA Ops:
  0.0 1.4 %crowded.1 = s32[1]{0:T(128)} custom-call(s32[3,32]{1,0:T(4,128)} %bitcast.4, s32[1,32]{1,0:T(1,128)} %bitcast.10, s32[3,32]{1,0:T(4,128)} %bitcast.7), custom_call_target="tpu_custom_call" | custom-call | tf_op jit(solution)/shard_map/crowded/pallas_call | solution.py:812
  2.1 41.3 %conditional.1 = (f32[1,1,2,384,384]{4,3,2,1,0:T(8,128)S(1)}) conditional(s32[]{:T(128)} %bitcast.3, (s32[3,32]{1,0:T(4,128)}, s32[32]{0:T(128)}, s32[3,32]{1,0:T(4,128)}, bf16[1,1,3,2,384,384]{5,4,3,2,1,0:T(8,128)(2,1)}, bf16[1,1,3,2,384,384]{5,4,3,2,1,0:T(8,128)(2,1)}, /*index=5*/bf16[1,1,2,384,384]{4,3,2,1,0:T(8,128)(2,1)}) %tuple.18, ...), branch_computations={%region_0.0_spmd, %region_1.0_spmd} | conditional | bytes 8 | solution.py:819
  2.1 41.1 %around.1 = f32[1,1,2,384,384]{4,3,2,1,0:T(8,128)S(1)} custom-call(s32[3,32]{1,0:T(4,128)} %get-tuple-element.32.off_hbm, s32[32]{0:T(128)} %get-tuple-element.33.count_hbm, s32[3,32]{1,0:T(4,128)} %get-tuple-element.34.range_hbm, bf16[1,1,3,2,384,384]{5,4,3,2,1,0:T(8,128)(2,1)} %get-tuple-element.35.green_hbm, ...), custom_call_target="tpu_custom_call" | custom-call | tf_op jit(solution)/shard_map/cond/branch_0_fun/around/pallas_call | solution.py:773
  43.4 1.0 %copy.12 = f32[1,1,2,384,384]{4,3,2,1,0:T(8,128)} copy(f32[1,1,2,384,384]{4,3,2,1,0:T(8,128)S(1)} %get-tuple-element.44) | data formatting | bytes 2359296

commit v5 on v4

--- a/solution.py
+++ b/solution.py
@@ -62,7 +62,8 @@
         above = jnp.concatenate([filled[:, HOP:], filled[:, :HOP]], axis=1)
         below = jnp.concatenate([filled[:, -HOP:], filled[:, :-HOP]], axis=1)
         relay = jnp.where(turned(slab, way) > 0, above, below)
-        stuck = (relay > SHARED) | jnp.logical_not(detours(slab, way, slabs))
+        room = jnp.where(filled > DIRECT + GROUP, SHARED, SHARED + GROUP)
+        stuck = (relay > room) | jnp.logical_not(detours(slab, way, slabs))
         crowded = crowded + ((filled > DIRECT) & stuck).astype(F32)
     out_ref[0] = jnp.max(crowded).astype(jnp.int32)
 
@@ -148,13 +149,12 @@
 
 
 def centre_plan(width):
-    chunks, whole = width // CHUNK, slice(None)
-    plan = [(whole, c * CHUNK, CHUNK) for c in range(chunks - 1)]
-    plan += [(whole, width - CHUNK, CHUNK - LAST)]
-    return plan + [(slice(c, c + 1), width - LAST, LAST) for c in range(chunks)]
-
-
-def finish(centre, comes, cent, b_v, side_v, y_v, part_v, acc_v, out_ref):
+    whole, half, most = slice(None), width // 2, width - LAST
+    plan = [(whole, 0, CHUNK), (whole, CHUNK, half - CHUNK), (whole, half, most - half)]
+    return plan + [(slice(c, c + 1), most, LAST) for c in range(width // CHUNK)]
+
+
+def finish(centre, comes, cent, late, b_v, side_v, y_v, part_v, acc_v, out_ref):
     width = acc_v.shape[0]
     chunks = width // CHUNK
     plan = centre_plan(width)
@@ -162,6 +162,8 @@
         rows = slice(row, row + count)
         final = n == len(plan) - 1
         complete = these == slice(None) or final
+        if row == width // 2:
+            late()
         for way in range(2):
             arrived(comes[way], centre[way][n])
             x = part_v[way, rows]
@@ -309,7 +311,7 @@
                     ]
             return carry
 
-        lax.fori_loop(first, last, step, 0)
+        lax.fori_loop(first, last, step, 0, unroll=4)
 
     for table in tables:
         table.wait()
@@ -374,7 +376,16 @@
                 part_v[way, rows] = x if slot == 0 else part_v[way, rows] + x
     centre = [copies[first_centre:] for copies in sent]
     finish(
-        centre, comes, lambda way, c, rows: got_v[way, 2, c, rows], b_v, side_v, y_v, part_v, acc_v, out_ref
+        centre,
+        comes,
+        lambda way, c, rows: got_v[way, 2, c, rows],
+        lambda: None,
+        b_v,
+        side_v,
+        y_v,
+        part_v,
+        acc_v,
+        out_ref,
     )
 
     gone(has_high, up)
@@ -513,7 +524,7 @@
         for h, these in enumerate(halves):
             spill[way].append(
                 remote(
-                    list_v.at[way, DIRECT + h * GROUP : DIRECT + (h + 1) * GROUP],
+                    list_v.at[way, LIST - (h + 1) * GROUP : LIST - h * GROUP],
                     spill_v.at[way, these],
                     spill_send.at[way, h],
                     spill_recv.at[way, h],
@@ -523,7 +534,7 @@
             returned[way].append(
                 remote(
                     got_v[way].at[SHARED + h * GROUP : SHARED + (h + 1) * GROUP],
-                    back_v[way].at[these],
+                    back_v[way].at[halves[1 - h]],
                     back_send.at[way, h],
                     back_recv.at[way, h],
                     handed[way] + (1, -1)[way],
@@ -575,7 +586,7 @@
                             mine_v[at, m, c, unit_rows, lanes] = value
             return carry
 
-        lax.fori_loop(first, last, step, 0)
+        lax.fori_loop(first, last, step, 0, unroll=4)
 
     def layout(slab, way):
         blocks = []
@@ -599,7 +610,7 @@
             list_v[way, p] = mine_v[at, row, col] * keep
             return carry
 
-        lax.fori_loop(first, last, step, 0)
+        lax.fori_loop(first, last, step, 0, unroll=4)
 
     for table in tables:
         table.wait()
@@ -688,16 +699,16 @@
             arrived(comes[way], direct[way][n])
             start(hands[way], returned[way][h])
 
-    def multiply(way, source, first, last, down_n, across_n, before, partner, fresh):
-        for m in range(width // UNIT):
+    def multiply(way, source, first, last, down_n, across_n, before, partner, fresh, top=0):
+        for m in range(top // UNIT, width // UNIT):
             for c in range(chunks):
                 position = before + m * across_n + c
                 there = (m < down_n) & (c < across_n) & (position >= first) & (position < last)
                 keep = jnp.where(there, 1.0, 0.0).astype(BF16)
                 position = jnp.clip(position - first, 0, last - first - 1)
                 block_v[c, m * UNIT : (m + 1) * UNIT] = source[position] * keep
-        for r in range(chunks):
-            rows = slice(r * CHUNK, (r + 1) * CHUNK)
+        for row in range(top, width, width // 2):
+            rows = slice(row, row + width // 2)
             x = None
             for c in range(chunks):
                 term = dot(block_v[c, rows], b_chunk(b_v, partner, c))
@@ -714,14 +725,26 @@
         arrived(comes[way], direct[way][0], direct[way][2])
         multiply(way, got_v[way], 0, DIRECT, down_a, across_a, 0, partner_a, True)
         multiply(way, got_v[way], 0, DIRECT, down_b, across_b, size_a, partner_b, False)
-    for way in range(2):
-        (_, _, size_a), (down_b, across_b, _) = blocks[way]
-        partner_b = (2, 0)[way]
-        arrived(gets[way], *returned[way])
-        multiply(way, back_v[way], DIRECT, LIST, down_b, across_b, size_a, partner_b, False)
+
+    def late():
+        for way in range(2):
+            (_, _, size_a), (down_b, across_b, _) = blocks[way]
+            arrived(gets[way], *returned[way])
+            multiply(
+                way, back_v[way], DIRECT, LIST, down_b, across_b, size_a, (2, 0)[way], False, width // 2
+            )
 
     finish(
-        centre, comes, lambda way, c, rows: cent_v[way, c, rows], b_v, side_v, y_v, part_v, acc_v, out_ref
+        centre,
+        comes,
+        lambda way, c, rows: cent_v[way, c, rows],
+        late,
+        b_v,
+        side_v,
+        y_v,
+        part_v,
+        acc_v,
+        out_ref,
     )
 
     gone(has_high, up)

time: 45.3 us -> 44.6 us (0.985); the launches traced: 44.4 us -> 44.5 us
  no operation moved by 1% of the time
where the time goes in v5:
time: 44.6 us; the launch traced here: 44.5 us
  Pallas kernels  42.6 us (96%)
  local copies, waits for them, and re-layouts  1.02 us (2%)
  between operations  0.67 us (2%)
    pallas_call x1, Pallas kernels, call(): pl.pallas_call(functools.partial(what, slabs, energies), out_shape=jax.Sh...  41.1 us
    pallas_call x1, Pallas kernels, body(): pl.pallas_call(crowded_kernel, out_shape=jax.ShapeDtypeStruct((1,), jnp.i...  1.44 us
    unnamed x1, local copies, waits for them, and re-layouts  1.02 us

profile of v5, /device:TPU:130, one launch (start us, length us, event | category | flops | bytes accessed | tf_op | source)
XLA Modules:
  0.0 44.5 jit_solution(10072699476081509794)
XLA Ops:
  0.0 1.4 %crowded.1 = s32[1]{0:T(128)} custom-call(s32[3,32]{1,0:T(4,128)} %bitcast.4, s32[1,32]{1,0:T(1,128)} %bitcast.10, s32[3,32]{1,0:T(4,128)} %bitcast.7), custom_call_target="tpu_custom_call" | custom-call | tf_op jit(solution)/shard_map/crowded/pallas_call | solution.py:835
  2.1 41.4 %conditional.1 = (f32[1,1,2,384,384]{4,3,2,1,0:T(8,128)S(1)}) conditional(s32[]{:T(128)} %bitcast.3, (s32[3,32]{1,0:T(4,128)}, s32[32]{0:T(128)}, s32[3,32]{1,0:T(4,128)}, bf16[1,1,3,2,384,384]{5,4,3,2,1,0:T(8,128)(2,1)}, bf16[1,1,3,2,384,384]{5,4,3,2,1,0:T(8,128)(2,1)}, /*index=5*/bf16[1,1,2,384,384]{4,3,2,1,0:T(8,128)(2,1)}) %tuple.18, ...), branch_computations={%region_0.0_spmd, %region_1.0_spmd} | conditional | bytes 8 | solution.py:842
  2.1 41.1 %around.1 = f32[1,1,2,384,384]{4,3,2,1,0:T(8,128)S(1)} custom-call(s32[3,32]{1,0:T(4,128)} %get-tuple-element.32.off_hbm, s32[32]{0:T(128)} %get-tuple-element.33.count_hbm, s32[3,32]{1,0:T(4,128)} %get-tuple-element.34.range_hbm, bf16[1,1,3,2,384,384]{5,4,3,2,1,0:T(8,128)(2,1)} %get-tuple-element.35.green_hbm, ...), custom_call_target="tpu_custom_call" | custom-call | tf_op jit(solution)/shard_map/cond/branch_0_fun/around/pallas_call | solution.py:796
  43.5 1.0 %copy.12 = f32[1,1,2,384,384]{4,3,2,1,0:T(8,128)} copy(f32[1,1,2,384,384]{4,3,2,1,0:T(8,128)S(1)} %get-tuple-element.44) | data formatting | bytes 2359296

commit v6 on v5

--- a/solution.py
+++ b/solution.py
@@ -48,7 +48,17 @@
     return relay + jnp.where(lax.rem(relay, HOP) == 1 + way, turn, -turn)
 
 
-def crowded_kernel(off_ref, count_ref, range_ref, out_ref):
+def crowded_kernel(off_hbm, count_hbm, range_hbm, out_ref, off_ref, count_ref, range_ref, sem):
+    tables = [
+        pltpu.make_async_copy(source, held, sem.at[n])
+        for n, (source, held) in enumerate(
+            ((off_hbm, off_ref), (count_hbm, count_ref), (range_hbm, range_ref))
+        )
+    ]
+    for table in tables:
+        table.start()
+    for table in tables:
+        table.wait()
     off, reach = off_ref[...], range_ref[...]
     slots, slabs = off.shape
     live = lax.broadcasted_iota(jnp.int32, off.shape, 0) < count_ref[...]
@@ -610,30 +620,29 @@
             list_v[way, p] = mine_v[at, row, col] * keep
             return carry
 
-        lax.fori_loop(first, last, step, 0, unroll=4)
+        lax.fori_loop(first, last, step, 0, unroll=3)
 
     for table in tables:
         table.wait()
     tiles = width // TILE // chunks
-    for way in range(2):
-        wanted = [(2 * way + n, OFFSETS[2 * way + n]) for n in range(2)]
-        if way == 0:
-            for c in range(chunks):
-                load_sigma[c].wait()
-                combine(wanted, False, c * tiles, (c + 1) * tiles)
-            load_green.start()
-        else:
-            combine(wanted, False)
-        pack(way, 0, LIST)
+    for c in range(chunks):
+        load_sigma[c].wait()
+        for way in range(2):
+            wanted = [(2 * way + n, OFFSETS[2 * way + n]) for n in range(2)]
+            combine(wanted, False, c * tiles, (c + 1) * tiles)
+    load_green.start()
+    for way in range(2):
+        pack(way, DIRECT, LIST)
+        pack(way, 0, 9)
         if way == 0:
             greeted(peers)
         start(sends[way], spill[way][0])
         start(goes[way], direct[way][0])
-        if way == 0:
-            start(has_high, up)
-            start(has_low, down)
+    start(has_high, up)
+    start(has_low, down)
     for way in range(2):
         start(sends[way], spill[way][1])
+        pack(way, 9, DIRECT)
 
     for way in range(2):
 
@@ -694,10 +703,16 @@
     merge(1)
     for way in range(2):
         start(goes[way], direct[way][3], *centre[way])
-    for n, h in ((1, 0), (3, 1)):
-        for way in range(2):
-            arrived(comes[way], direct[way][n])
-            start(hands[way], returned[way][h])
+    first_row = lax.rem(k, HOP) == 0
+    for order, here in (((1, 0), first_row), ((0, 1), jnp.logical_not(first_row))):
+
+        @pl.when(here)
+        def _():
+            for n, h in ((1, 0), (3, 1)):
+                for way in order:
+                    arrived(comes[way], direct[way][n])
+                    start(hands[way], returned[way][h])
+
 
     def multiply(way, source, first, last, down_n, across_n, before, partner, fresh, top=0):
         for m in range(top // UNIT, width // UNIT):
@@ -835,10 +850,16 @@
         crowded = pl.pallas_call(
             crowded_kernel,
             out_shape=jax.ShapeDtypeStruct((1,), jnp.int32),
-            in_specs=[vmem] * 3,
+            in_specs=[hbm] * 3,
             out_specs=pl.BlockSpec(memory_space=pltpu.SMEM),
+            scratch_shapes=[
+                pltpu.VMEM((slots, slabs), jnp.int32),
+                pltpu.VMEM((1, slabs), jnp.int32),
+                pltpu.VMEM((slots, slabs), jnp.int32),
+                pltpu.SemaphoreType.DMA((3,)),
+            ],
             name="crowded",
-        )(pair_off.T, pair_count[None], pair_range.T)
+        )(operands[0], pltpu.with_memory_space_constraint(pair_count[None], pltpu.HBM), operands[2])
         return lax.cond(crowded[0] > 0, straight, around, *operands)
 
     wide = P("energy", "slab", None, None, None, None)

time: 44.6 us -> 45.4 us (1.018)
  Pallas kernels: 42.6 us -> 43.3 us
    pallas_call x1, Pallas kernels: 41.1 us -> 41.8 us  [call(): pl.pallas_call(functools.partial(what, slabs, energies), out_shape=jax.Sh...]
where the time goes in v6:
time: 45.4 us; the launch traced here: 45.2 us
  Pallas kernels  43.3 us (95%)
  local copies, waits for them, and re-layouts  1.02 us (2%)
  between operations  0.67 us (1%)
    pallas_call x1, Pallas kernels, call(): pl.pallas_call(functools.partial(what, slabs, energies), out_shape=jax.Sh...  41.8 us
    pallas_call x1, Pallas kernels, body(): pl.pallas_call(crowded_kernel, out_shape=jax.ShapeDtypeStruct((1,), jnp.i...  1.47 us
    unnamed x1, local copies, waits for them, and re-layouts  1.02 us

profile of v6, /device:TPU:130, one launch (start us, length us, event | category | flops | bytes accessed | tf_op | source)
XLA Modules:
  0.0 45.2 jit_solution(6470091996168175427)
XLA Ops:
  0.0 1.5 %crowded.1 = s32[1]{0:T(128)} custom-call(s32[3,32]{1,0:T(4,128)} %bitcast.4, s32[1,32]{1,0:T(1,128)} %bitcast.10, s32[3,32]{1,0:T(4,128)} %bitcast.7), custom_call_target="tpu_custom_call" | custom-call | tf_op jit(solution)/shard_map/crowded/pallas_call | solution.py:850
  2.1 42.1 %conditional.1 = (f32[1,1,2,384,384]{4,3,2,1,0:T(8,128)S(1)}) conditional(s32[]{:T(128)} %bitcast.3, (s32[3,32]{1,0:T(4,128)}, s32[32]{0:T(128)}, s32[3,32]{1,0:T(4,128)}, bf16[1,1,3,2,384,384]{5,4,3,2,1,0:T(8,128)(2,1)}, bf16[1,1,3,2,384,384]{5,4,3,2,1,0:T(8,128)(2,1)}, /*index=5*/bf16[1,1,2,384,384]{4,3,2,1,0:T(8,128)(2,1)}) %tuple.18, ...), branch_computations={%region_0.0_spmd, %region_1.0_spmd} | conditional | bytes 8 | solution.py:863
  2.1 41.8 %around.1 = f32[1,1,2,384,384]{4,3,2,1,0:T(8,128)S(1)} custom-call(s32[3,32]{1,0:T(4,128)} %get-tuple-element.32.off_hbm, s32[32]{0:T(128)} %get-tuple-element.33.count_hbm, s32[3,32]{1,0:T(4,128)} %get-tuple-element.34.range_hbm, bf16[1,1,3,2,384,384]{5,4,3,2,1,0:T(8,128)(2,1)} %get-tuple-element.35.green_hbm, ...), custom_call_target="tpu_custom_call" | custom-call | tf_op jit(solution)/shard_map/cond/branch_0_fun/around/pallas_call | solution.py:811
  44.2 1.0 %copy.12 = f32[1,1,2,384,384]{4,3,2,1,0:T(8,128)} copy(f32[1,1,2,384,384]{4,3,2,1,0:T(8,128)S(1)} %get-tuple-element.44) | data formatting | bytes 2359296

commit v7 on v5

--- a/solution.py
+++ b/solution.py
@@ -682,6 +682,15 @@
                 term = dot(mine_v[at, these, c].reshape(width // 2, 2 * CHUNK), b_chunk(b_v, partner, c))
                 x = term if x is None else x + term
             part_v[0, rows] = x if n == 0 else part_v[0, rows] + x
+    merge(1)
+    for way in range(2):
+        start(goes[way], direct[way][3], *centre[way])
+    def hand_back(n, h):
+        for way in range(2):
+            arrived(comes[way], direct[way][n])
+            start(hands[way], returned[way][h])
+
+    hand_back(1, 0)
     for r in range(chunks):
         rows = slice(r * CHUNK, (r + 1) * CHUNK)
         x = part_v[0, rows]
@@ -691,13 +700,7 @@
         term = dot(a_v[r], y_v[: 2 * CHUNK])
         acc_v[...] = term if r == 0 else acc_v[...] + term
 
-    merge(1)
-    for way in range(2):
-        start(goes[way], direct[way][3], *centre[way])
-    for n, h in ((1, 0), (3, 1)):
-        for way in range(2):
-            arrived(comes[way], direct[way][n])
-            start(hands[way], returned[way][h])
+    hand_back(3, 1)
 
     def multiply(way, source, first, last, down_n, across_n, before, partner, fresh, top=0):
         for m in range(top // UNIT, width // UNIT):

time: 44.6 us -> 44.6 us (level)
  no operation moved by 1% of the time
where the time goes in v7:
time: 44.6 us; the launch traced here: 44.5 us
  Pallas kernels  42.6 us (96%)
  local copies, waits for them, and re-layouts  1.02 us (2%)
  between operations  0.67 us (2%)
    pallas_call x1, Pallas kernels, call(): pl.pallas_call(functools.partial(what, slabs, energies), out_shape=jax.Sh...  41.1 us
    pallas_call x1, Pallas kernels, body(): pl.pallas_call(crowded_kernel, out_shape=jax.ShapeDtypeStruct((1,), jnp.i...  1.44 us
    unnamed x1, local copies, waits for them, and re-layouts  1.02 us

profile of v7, /device:TPU:130, one launch (start us, length us, event | category | flops | bytes accessed | tf_op | source)
XLA Modules:
  0.0 44.5 jit_solution(12874569910492843198)
XLA Ops:
  0.0 1.4 %crowded.1 = s32[1]{0:T(128)} custom-call(s32[3,32]{1,0:T(4,128)} %bitcast.4, s32[1,32]{1,0:T(1,128)} %bitcast.10, s32[3,32]{1,0:T(4,128)} %bitcast.7), custom_call_target="tpu_custom_call" | custom-call | tf_op jit(solution)/shard_map/crowded/pallas_call | solution.py:838
  2.1 41.4 %conditional.1 = (f32[1,1,2,384,384]{4,3,2,1,0:T(8,128)S(1)}) conditional(s32[]{:T(128)} %bitcast.3, (s32[3,32]{1,0:T(4,128)}, s32[32]{0:T(128)}, s32[3,32]{1,0:T(4,128)}, bf16[1,1,3,2,384,384]{5,4,3,2,1,0:T(8,128)(2,1)}, bf16[1,1,3,2,384,384]{5,4,3,2,1,0:T(8,128)(2,1)}, /*index=5*/bf16[1,1,2,384,384]{4,3,2,1,0:T(8,128)(2,1)}) %tuple.18, ...), branch_computations={%region_0.0_spmd, %region_1.0_spmd} | conditional | bytes 8 | solution.py:845
  2.1 41.1 %around.1 = f32[1,1,2,384,384]{4,3,2,1,0:T(8,128)S(1)} custom-call(s32[3,32]{1,0:T(4,128)} %get-tuple-element.32.off_hbm, s32[32]{0:T(128)} %get-tuple-element.33.count_hbm, s32[3,32]{1,0:T(4,128)} %get-tuple-element.34.range_hbm, bf16[1,1,3,2,384,384]{5,4,3,2,1,0:T(8,128)(2,1)} %get-tuple-element.35.green_hbm, ...), custom_call_target="tpu_custom_call" | custom-call | tf_op jit(solution)/shard_map/cond/branch_0_fun/around/pallas_call | solution.py:799
  43.5 1.0 %copy.12 = f32[1,1,2,384,384]{4,3,2,1,0:T(8,128)} copy(f32[1,1,2,384,384]{4,3,2,1,0:T(8,128)S(1)} %get-tuple-element.44) | data formatting | bytes 2359296

commit v8 on v7

--- a/solution.py
+++ b/solution.py
@@ -441,7 +441,7 @@
     k = lax.axis_index("slab")
     e = lax.axis_index("energy")
     width = green_v.shape[-1]
-    slots = sigma_v.shape[0]
+    slots = sigma_v.shape[2]
     chunks = width // CHUNK
     has_low, has_high = e > 0, e < energies - 1
 
@@ -454,13 +454,16 @@
         )
     ]
     load_sigma = []
-    for c in range(chunks):
-        rows = slice(c * CHUNK, (c + 1) * CHUNK)
-        load_sigma.append(
-            pltpu.make_async_copy(
-                sigma_hbm.at[0, 0, :, :, rows], sigma_v.at[:, :, rows], local_sem.at[4 + c]
-            )
-        )
+    for m in range(width // UNIT):
+        for c in range(chunks):
+            rows, columns = slice(m * UNIT, (m + 1) * UNIT), slice(c * CHUNK, (c + 1) * CHUNK)
+            load_sigma.append(
+                pltpu.make_async_copy(
+                    sigma_hbm.at[0, 0, :, :, rows, columns],
+                    sigma_v.at[m, c],
+                    local_sem.at[4 + len(load_sigma)],
+                )
+            )
     load_green = pltpu.make_async_copy(green_hbm.at[0, 0], green_v, local_sem.at[3])
     peers = (
         (has_left, {"slab": k - 1}),
@@ -555,38 +558,47 @@
         live = (q < count_ref[slab]) & (off_ref[q, slab] == offset)
         return jnp.where(live, range_ref[q, slab], 0)
 
-    def combine(wanted, with_phonon, first=0, last=width // TILE):
-        reach = [[live_reach(k, q, offset) for q in range(slots)] for _, offset in wanted]
-
-        def step(t, carry):
-            rows = pl.ds(pl.multiple_of(t * TILE, TILE), TILE)
-            col_ids = lax.broadcasted_iota(jnp.int32, (TILE, width), 1)
-            m = lax.div(t, UNIT // TILE)
-            unit_rows = pl.ds(pl.multiple_of(t * TILE - m * UNIT, TILE), TILE)
-            inside = [
-                [col_ids < jnp.where(t * TILE < reach[n][q], reach[n][q], 0) for q in range(slots)]
-                for n in range(len(wanted))
-            ]
-            for part in range(2):
-                terms = [sigma_v[q, part, rows, :].astype(F32) for q in range(slots)]
-                for n, (at, _) in enumerate(wanted):
-                    kept = [jnp.where(inside[n][q], terms[q], 0.0) for q in range(slots)]
-                    total = functools.reduce(jnp.add, kept)
-                    if with_phonon:
-                        low = near_v[0, part, rows, :].astype(F32)
-                        high = near_v[1, part, rows, :].astype(F32)
-                        total = total + (0.5 * (low + high)).astype(BF16).astype(F32)
-                    total = total.astype(BF16)
-                    lanes = slice(part * CHUNK, (part + 1) * CHUNK)
-                    for c in range(chunks):
-                        value = total[:, c * CHUNK : (c + 1) * CHUNK]
-                        if with_phonon:
-                            own_v[c, rows, lanes] = value
-                        else:
-                            mine_v[at, m, c, unit_rows, lanes] = value
+    def unit_sum(m, c, reach):
+        column = c * CHUNK + lax.broadcasted_iota(jnp.int32, (UNIT, CHUNK), 1)
+        inside = [column < jnp.where(m * UNIT < reach[q], reach[q], 0) for q in range(slots)]
+        return [
+            functools.reduce(
+                jnp.add,
+                [jnp.where(inside[q], sigma_v[m, c, q, part].astype(F32), 0.0) for q in range(slots)],
+            )
+            for part in range(2)
+        ]
+
+    def reaches(offset):
+        return [live_reach(k, q, offset) for q in range(slots)]
+
+    def sum_sides():
+        wanted = [reaches(-1), reaches(1)]
+
+        def step(m, carry):
+            for c in range(chunks):
+                for at in range(2):
+                    for part, value in enumerate(unit_sum(m, c, wanted[at])):
+                        mine_v[at, m, c, :, part * CHUNK : (part + 1) * CHUNK] = value.astype(BF16)
             return carry
 
-        lax.fori_loop(first, last, step, 0, unroll=4)
+        lax.fori_loop(0, width // UNIT, step, 0)
+
+    def sum_own():
+        reach = reaches(0)
+
+        def step(m, carry):
+            rows = pl.ds(pl.multiple_of(m * UNIT, UNIT), UNIT)
+            for c in range(chunks):
+                columns = slice(c * CHUNK, (c + 1) * CHUNK)
+                for part, value in enumerate(unit_sum(m, c, reach)):
+                    low = near_v[0, part, rows, columns].astype(F32)
+                    high = near_v[1, part, rows, columns].astype(F32)
+                    value = value + (0.5 * (low + high)).astype(BF16).astype(F32)
+                    own_v[c, rows, part * CHUNK : (part + 1) * CHUNK] = value.astype(BF16)
+            return carry
+
+        lax.fori_loop(0, width // UNIT, step, 0)
 
     def layout(slab, way):
         blocks = []
@@ -597,6 +609,7 @@
 
     def pack(way, first, last):
         (_, across_a, size_a), (_, across_b, size_b) = layout(k, way)
+        reach_a, reach_b = [reaches(offset) for offset in OFFSETS[2 * way : 2 * way + 2]]
 
         def step(p, carry):
             in_a = p < size_a
@@ -605,35 +618,34 @@
             row = jnp.where(across == 3, lax.div(unit, 3), jnp.where(across == 2, lax.div(unit, 2), unit))
             col = jnp.clip(unit - row * across, 0, chunks - 1)
             row = jnp.clip(row, 0, width // UNIT - 1)
-            at = 2 * way + jnp.where(in_a, 0, 1)
-            keep = jnp.where(p < size_a + size_b, 1.0, 0.0).astype(BF16)
-            list_v[way, p] = mine_v[at, row, col] * keep
+            used = p < size_a + size_b
+            reach = [
+                jnp.where(used, jnp.where(in_a, reach_a[q], reach_b[q]), 0) for q in range(slots)
+            ]
+            for part, value in enumerate(unit_sum(row, col, reach)):
+                list_v[way, p, :, part * CHUNK : (part + 1) * CHUNK] = value.astype(BF16)
             return carry
 
-        lax.fori_loop(first, last, step, 0, unroll=4)
+        lax.fori_loop(first, last, step, 0, unroll=3)
 
     for table in tables:
         table.wait()
-    tiles = width // TILE // chunks
-    for way in range(2):
-        wanted = [(2 * way + n, OFFSETS[2 * way + n]) for n in range(2)]
-        if way == 0:
-            for c in range(chunks):
-                load_sigma[c].wait()
-                combine(wanted, False, c * tiles, (c + 1) * tiles)
-            load_green.start()
-        else:
-            combine(wanted, False)
-        pack(way, 0, LIST)
+    for load in load_sigma:
+        load.wait()
+    load_green.start()
+    for way in range(2):
+        pack(way, 0, 9)
         if way == 0:
             greeted(peers)
+        start(goes[way], direct[way][0])
+    for way in range(2):
+        pack(way, DIRECT, LIST)
         start(sends[way], spill[way][0])
-        start(goes[way], direct[way][0])
-        if way == 0:
-            start(has_high, up)
-            start(has_low, down)
+    start(has_high, up)
+    start(has_low, down)
     for way in range(2):
         start(sends[way], spill[way][1])
+        pack(way, 9, DIRECT)
 
     for way in range(2):
 
@@ -656,12 +668,13 @@
         def _():
             near_v[slot] = jnp.zeros_like(near_v[slot])
 
+    sum_sides()
     load_green.wait()
     prepare(green_v, b_v, a_v, side_v)
 
     arrived(has_low, up)
     arrived(has_high, down)
-    combine([(4, 0)], True)
+    sum_own()
 
     def merge(h):
         for way in range(2):
@@ -673,7 +686,7 @@
     for way in range(2):
         start(goes[way], direct[way][1], direct[way][2])
 
-    for n, (at, partner) in enumerate(((2, 0), (0, 2))):
+    for at, partner in enumerate((0, 2)):
         for r in range(2):
             rows = slice(r * width // 2, (r + 1) * width // 2)
             these = slice(rows.start // UNIT, rows.stop // UNIT)
@@ -681,7 +694,7 @@
             for c in range(chunks):
                 term = dot(mine_v[at, these, c].reshape(width // 2, 2 * CHUNK), b_chunk(b_v, partner, c))
                 x = term if x is None else x + term
-            part_v[0, rows] = x if n == 0 else part_v[0, rows] + x
+            part_v[0, rows] = x if at == 0 else part_v[0, rows] + x
     merge(1)
     for way in range(2):
         start(goes[way], direct[way][3], *centre[way])
@@ -777,9 +790,8 @@
             pltpu.SMEM((slabs,), jnp.int32),
             pltpu.SMEM((slots, slabs), jnp.int32),
             pltpu.VMEM((3, 2, width, width), BF16),
-            pltpu.VMEM((slots, 2, width, width), BF16),
-            pltpu.VMEM((2, 2, width, width), BF16),
         ]
+        near = pltpu.VMEM((2, 2, width, width), BF16)
         factors = [
             pltpu.VMEM((3, 2 * width, 2 * width), BF16),
             pltpu.VMEM(split, BF16),
@@ -787,7 +799,7 @@
             pltpu.VMEM((4 * CHUNK, 2 * width), BF16),
             pltpu.VMEM((2, width, 2 * width), F32),
             pltpu.VMEM((width, 2 * width), F32),
-            pltpu.SemaphoreType.DMA((4 + chunks,)),
+            pltpu.SemaphoreType.DMA((4 + chunks * (width // UNIT),)),
             pltpu.SemaphoreType.DMA((2,)),
             pltpu.SemaphoreType.DMA((2,)),
         ]
@@ -813,7 +825,12 @@
             straight_kernel,
             0,
             "straight",
-            [pltpu.VMEM((5,) + split, BF16), pltpu.VMEM((2, 3) + split, BF16)],
+            [
+                pltpu.VMEM((slots, 2, width, width), BF16),
+                near,
+                pltpu.VMEM((5,) + split, BF16),
+                pltpu.VMEM((2, 3) + split, BF16),
+            ],
             flags(chunks + 1 + pieces),
         )
         around = functools.partial(
@@ -822,7 +839,9 @@
             1,
             "around",
             [
-                pltpu.VMEM((4, width // UNIT, chunks) + unit, BF16),
+                pltpu.VMEM((width // UNIT, chunks, slots, 2, UNIT, CHUNK), BF16),
+                near,
+                pltpu.VMEM((2, width // UNIT, chunks) + unit, BF16),
                 pltpu.VMEM(split, BF16),
                 pltpu.VMEM((2, LIST) + unit, BF16),
                 pltpu.VMEM((DIRECT,) + unit, BF16),

time: 44.6 us -> 45.2 us (1.013); the launches traced: 44.5 us -> 44.6 us
  no operation moved by 1% of the time
where the time goes in v8:
time: 45.2 us; the launch traced here: 44.6 us
  Pallas kernels  42.7 us (94%)
  local copies, waits for them, and re-layouts  1.02 us (2%)
  between operations  0.67 us (1%)
    pallas_call x1, Pallas kernels, call(): pl.pallas_call(functools.partial(what, slabs, energies), out_shape=jax.Sh...  41.3 us
    pallas_call x1, Pallas kernels, body(): pl.pallas_call(crowded_kernel, out_shape=jax.ShapeDtypeStruct((1,), jnp.i...  1.44 us
    unnamed x1, local copies, waits for them, and re-layouts  1.02 us

profile of v8, /device:TPU:130, one launch (start us, length us, event | category | flops | bytes accessed | tf_op | source)
XLA Modules:
  0.0 44.6 jit_solution(4730477528119487117)
XLA Ops:
  0.0 1.4 %crowded.1 = s32[1]{0:T(128)} custom-call(s32[3,32]{1,0:T(4,128)} %bitcast.4, s32[1,32]{1,0:T(1,128)} %bitcast.10, s32[3,32]{1,0:T(4,128)} %bitcast.7), custom_call_target="tpu_custom_call" | custom-call | tf_op jit(solution)/shard_map/crowded/pallas_call | solution.py:857
  2.1 41.5 %conditional.1 = (f32[1,1,2,384,384]{4,3,2,1,0:T(8,128)S(1)}) conditional(s32[]{:T(128)} %bitcast.3, (s32[3,32]{1,0:T(4,128)}, s32[32]{0:T(128)}, s32[3,32]{1,0:T(4,128)}, bf16[1,1,3,2,384,384]{5,4,3,2,1,0:T(8,128)(2,1)}, bf16[1,1,3,2,384,384]{5,4,3,2,1,0:T(8,128)(2,1)}, /*index=5*/bf16[1,1,2,384,384]{4,3,2,1,0:T(8,128)(2,1)}) %tuple.18, ...), branch_computations={%region_0.0_spmd, %region_1.0_spmd} | conditional | bytes 8 | solution.py:864
  2.1 41.3 %around.1 = f32[1,1,2,384,384]{4,3,2,1,0:T(8,128)S(1)} custom-call(s32[3,32]{1,0:T(4,128)} %get-tuple-element.32.off_hbm, s32[32]{0:T(128)} %get-tuple-element.33.count_hbm, s32[3,32]{1,0:T(4,128)} %get-tuple-element.34.range_hbm, bf16[1,1,3,2,384,384]{5,4,3,2,1,0:T(8,128)(2,1)} %get-tuple-element.35.green_hbm, ...), custom_call_target="tpu_custom_call" | custom-call | tf_op jit(solution)/shard_map/cond/branch_0_fun/around/pallas_call | solution.py:811
  43.6 1.0 %copy.12 = f32[1,1,2,384,384]{4,3,2,1,0:T(8,128)} copy(f32[1,1,2,384,384]{4,3,2,1,0:T(8,128)S(1)} %get-tuple-element.44) | data formatting | bytes 2359296
